TPU v7x, 512 devices: a whole 4x8x8 slice. The times are simulated.
512 devices in a mesh: layer: 16 (over y, core), row: 4 (over x), col: 8 (over z).
Axes of the slice: x: 4, y: 8, z: 8, core: 2. Of those that a mesh axis runs over, the one named last changes fastest.
Arguments:
- left: float32 [2048, 4096], P('row', ('layer', 'col')), may hold values from -6 to 6
- right: float32 [4096, 32768], P(('layer', 'row'), 'col'), may hold values from -0.09375 to 0.09375
Outputs:
- product: float32 [2048, 32768], P(('row', 'layer'), 'col')
All inputs are finite; a program needn't handle non-finite values.
Results may differ from a plain program's by a relative error of at most 0.000076.
Values sent between devices are 32-bit elements; how exact they have to be, the bound alone decides.
No kernel may reach another device: no remote copies, remote signals or barrier semaphores. Data moves between devices by JAX's collectives and lax.ppermute only.
A program may use at most 128 MiB of HBM per device.

v0:
```python
import jax
import jax.numpy as jnp
from jax import lax
from jax.sharding import PartitionSpec as P


def sent_to_all(shard, axis):
    copies = jnp.broadcast_to(shard, (lax.axis_size(axis), *shard.shape))
    return lax.all_to_all(copies, axis, split_axis=0, concat_axis=0, tiled=True)


def in_order(parts, dim):
    dims = list(parts.shape[1:])
    dims[dim] *= parts.shape[0]
    return jnp.moveaxis(parts, 0, dim).reshape(dims)


def gathered_copies(shard, axis, dim):
    parts = sent_to_all(shard, axis)
    return in_order(parts, dim)


def body(left, right):
    panel = lax.all_gather(left, "col", axis=1, tiled=True)
    operand = gathered_copies(right, "row", 0)
    partial_value = jnp.dot(
        panel, operand, precision=lax.Precision.HIGHEST, preferred_element_type=jnp.float32
    )
    return lax.psum_scatter(partial_value, "layer", scatter_dimension=0, tiled=True)


def solution(mesh):
    in_specs = (P("row", ("layer", "col")), P(("layer", "row"), "col"))
    out_specs = P(("row", "layer"), "col")
    return jax.shard_map(body, mesh=mesh, in_specs=in_specs, out_specs=out_specs, check_vma=False)
```

profile of v0, /device:TPU:29, one launch (start us, length us, event | category | flops | bytes accessed | tf_op | source)
XLA Modules:
  0.0 158.1 jit_solution(16214954873665577412)
XLA Ops:
  6.5 3.7 %broadcast_in_dim.3 = f32[4,64,4096]{2,1,0:T(8,128)} broadcast(f32[64,4096]{1,0:T(8,128)} %param.3), dimensions={1,2} | broadcast | bytes 5242880 | tf_op jit(solution)/shard_map/broadcast_in_dim | solution.py:8
  10.2 0.0 copy-start
  10.2 5.2 %all-to-all-start = ((f32[4,64,4096]{2,1,0:T(8,128)}), f32[4,64,4096]{2,1,0:T(8,128)}, u32[]{:S(2)}, u32[]{:S(2)}) async-start(f32[4,64,4096]{2,1,0:T(8,128)} %broadcast_in_dim.3), calls=%async_computation | async-start | bytes 8388608 | tf_op jit(solution)/shard_map/all_to_all | solution.py:9
  15.5 0.0 reduce-scatter.2.cloned.1.call-start
  15.5 0.0 copy-done
  15.5 26.0 %all_gather.3 = f32[512,256]{0,1:T(8,128)S(1)} all-gather(f32[512,32]{0,1:T(8,128)S(1)} %copy-done), channel_id=1, replica_groups=mesh['layer'=16,'row'=4,'col'=8] {'col'}, dimensions={1}, use_global_device_ids=true | all-gather | bytes 589824 | tf_op jit(solution)/shard_map/all_gather | solution.py:24
  41.5 19.7 %all-to-all-done = f32[4,64,4096]{2,1,0:T(8,128)} async-done(((f32[4,64,4096]{2,1,0:T(8,128)}), f32[4,64,4096]{2,1,0:T(8,128)}, u32[]{:S(2)}, u32[]{:S(2)}) %all-to-all-start) | async-done | bytes 4194336 | tf_op jit(solution)/shard_map/all_to_all | solution.py:9
  61.2 10.6 %fusion = f32[512,4096]{1,0:T(8,128)} fusion(f32[512,256]{0,1:T(8,128)S(1)} %all_gather.3, f32[256,4096]{1,0:T(8,128)} %bitcast), kind=kOutput, calls=%fused_computation | convolution fusion | flops 6442450944 | bytes 13107200 | tf_op jit(solution)/shard_map/dot_general | solution.py:26
  71.8 0.0 reduce-scatter.2.cloned.1.call-update
  71.8 79.4 %reduce-scatter.2.cloned.1.call-done = f32[32,4096]{1,0:T(8,128)} async-done(((f32[512,4096]{1,0:T(8,128)}), f32[32,4096]{1,0:T(8,128)}) %reduce-scatter.2.cloned.1.call-update) | async-done | bytes 524304 | tf_op jit(solution)/shard_map/reduce_scatter | solution.py:29
Async XLA Ops:
  10.2 5.2 %copy-start = (f32[512,32]{0,1:T(8,128)S(1)}, f32[512,32]{0,1:T(8,128)}, u32[]{:S(2)}) copy-start(f32[512,32]{0,1:T(8,128)} %param.2) | copy-start | bytes 196612
  10.2 50.9 %all-to-all-start = ((f32[4,64,4096]{2,1,0:T(8,128)}), f32[4,64,4096]{2,1,0:T(8,128)}, u32[]{:S(2)}, u32[]{:S(2)}) async-start(f32[4,64,4096]{2,1,0:T(8,128)} %broadcast_in_dim.3), calls=%async_computation | async-start | bytes 8388608 | tf_op jit(solution)/shard_map/all_to_all | solution.py:9
  15.5 135.8 %reduce-scatter.2.cloned.1.call-start = ((), (), s32[]{:S(2)}) async-start(), calls=%async_computation.2 | async-start | bytes 8912896 | tf_op jit(solution)/shard_map/reduce_scatter | solution.py:29
Sparse Core Ops, SparseCore 0:
  72.0 79.2 reduce-scatter.1
where the time goes:
time: 158 us
  waiting for transfers between devices  99.2 us (63%)
  blocking collectives  26 us (16%)
  between operations  13.4 us (8%)
  matrix products  10.6 us (7%)
  starting transfers between devices  5.24 us (3%)
  local copies, waits for them, and re-layouts  3.7 us (2%)
    reduce_scatter x1, waiting for transfers between devices, body(): lax.psum_scatter(partial_value, 'layer', scatter_dimension=0, tiled=True)  79.4 us
    all_gather x1, blocking collectives, body(): panel = lax.all_gather(left, 'col', axis=1, tiled=True)  26 us
    all_to_all x1, waiting for transfers between devices, sent_to_all(): return lax.all_to_all(copies, axis, split_axis=0, concat_axis=0, tiled=True)  19.7 us
    dot_general x1, matrix products, body(): jnp.dot(panel, operand, precision=lax.Precision.HIGHEST, preferred_elemen...  10.6 us
    all_to_all x1, starting transfers between devices, sent_to_all(): return lax.all_to_all(copies, axis, split_axis=0, concat_axis=0, tiled=True)  5.24 us
    broadcast_in_dim x1, local copies, waits for them, and re-layouts, sent_to_all(): copies = jnp.broadcast_to(shard, (lax.axis_size(axis), *shard.shape))  3.7 us
  transfers between devices with their start and end apart: 2, of which 2 were waited for; matrix products, arithmetic and copies ran while one was open for 0% of the time, Pallas kernels for 0%

commit v1 on v0

v1 whole, which is shorter than its diff:
```python
import jax
import jax.numpy as jnp
from jax import lax
from jax.sharding import PartitionSpec as P


def dot(a, b):
    return lax.dot_general(
        a,
        b,
        (((0,), (0,)), ((), ())),
        precision=lax.Precision.HIGH,
        preferred_element_type=jnp.float32,
    )


def body(left, right):
    layers, rows = lax.axis_size("layer"), lax.axis_size("row")
    cols = lax.axis_size("col")
    ys = layers // 2
    layer, x = lax.axis_index("layer"), lax.axis_index("row")
    y, c = layer // 2, layer % 2
    n = x % 2
    width = right.shape[1] // 2
    depth = left.shape[1]
    height = left.shape[0] // layers

    swap_core = [(i, i ^ 1) for i in range(layers)]
    swap_pair = [(i, i ^ 1) for i in range(rows)]
    swap_both = [
        (i * rows + j, (i ^ 1) * rows + (j ^ 1))
        for i in range(layers)
        for j in range(rows)
    ]
    onward = [(2 * i, 2 * ((i + 1) % ys)) for i in range(ys)]
    onward += [(2 * i + 1, 2 * ((i - 1) % ys) + 1) for i in range(ys)]

    def block_of(slot, core):
        away = jnp.where(slot == 0, 4, jnp.where(slot == 7, 0, 3 - (slot - 1) // 2))
        half = jnp.where((slot == 0) | (slot == 7), core, core ^ ((slot + 1) % 2))
        return ((y + (1 - 2 * core) * away) % ys) * 2 + half

    slots = 8
    count = slots * height
    lane = lax.broadcasted_iota(jnp.int32, (left.shape[0], 2 * count), 1)
    source = lax.broadcasted_iota(jnp.int32, (left.shape[0], 2 * count), 0)
    core = jnp.where(lane < count, c, 1 - c)
    slot = (lane // height) % slots
    wanted = block_of(slot, core) * height + lane % height
    picked = lax.dot_general(
        left,
        (source == wanted).astype(jnp.float32),
        (((0,), (0,)), ((), ())),
        precision=lax.Precision.HIGHEST,
    )
    mine, theirs = picked[:, :count], picked[:, count:]
    both = jnp.concatenate([mine, lax.ppermute(theirs, "layer", swap_core)], 0)

    keep = lax.dynamic_slice_in_dim(right, n * width, width, 1)
    give = lax.dynamic_slice_in_dim(right, (1 - n) * width, width, 1)
    step = [(i, (i + 1) % rows) for i in range(rows)]
    from_low = lax.ppermute(give, "row", step)
    from_high = lax.ppermute(give, "row", [(j, i) for i, j in step])
    from_far = lax.ppermute(keep, "row", [(i, (i + 2) % rows) for i in range(rows)])
    own_b = jnp.concatenate([keep, from_low, from_high, from_far], 0)
    other_b = lax.ppermute(own_b, "layer", swap_core)

    spread = jnp.broadcast_to(both[None], (cols,) + both.shape)
    full = lax.all_to_all(spread, "col", split_axis=0, concat_axis=0, tiled=True)
    full = full.reshape(rows, cols // rows, 2, depth, count)

    def ordered(part, at):
        order = [at, at - 1, at + 1, at + 2]
        part = jnp.stack(
            [lax.dynamic_index_in_dim(part, i % rows, 0, keepdims=False) for i in order]
        )
        part = part.transpose(2, 0, 1, 3, 4)
        return part.reshape(2, cols * depth, part.shape[-1])

    first = 3 * height
    early, late = full[..., :first], full[..., first:]
    early_pair = lax.ppermute(ordered(early, x ^ 1), "row", swap_pair)
    late_pair = lax.ppermute(ordered(late, x ^ 1), "row", swap_pair)
    early, late = ordered(early, x), ordered(late, x)

    def product(a):
        return dot(a[0], own_b) + dot(a[1], other_b)

    def reduce(near, far):
        near_p = product(near)
        total = lax.ppermute(near_p[:height], "layer", onward)
        total = jnp.concatenate(
            [near_p[height : 2 * height] + total, near_p[2 * height :]], 0
        )
        far_p = product(far)
        total = lax.ppermute(total, "layer", onward)
        total = lax.ppermute(total + far_p[: 2 * height], "layer", onward)
        total = lax.ppermute(total + far_p[2 * height : 4 * height], "layer", onward)
        return total[:height] + far_p[4 * height :], total[height:]

    self_own, self_other = reduce(early, late)
    pair_own, pair_other = reduce(early_pair, late_pair)
    in_core = lax.ppermute(self_other, "layer", swap_core)
    in_pair = lax.ppermute(pair_own, "row", swap_pair)
    in_both = lax.ppermute(pair_other, ("layer", "row"), swap_both)
    here = self_own + in_core
    there = in_pair + in_both
    return jnp.concatenate(
        [jnp.where(n == 0, here, there), jnp.where(n == 0, there, here)], 1
    )


def solution(mesh):
    in_specs = (P("row", ("layer", "col")), P(("layer", "row"), "col"))
    out_specs = P(("row", "layer"), "col")
    return jax.shard_map(
        body, mesh=mesh, in_specs=in_specs, out_specs=out_specs, check_vma=False
    )
```

time: 158 us -> 126 us (0.80)
  the two profiles are of different devices: /device:TPU:29 before, /device:TPU:1 now
where the time goes in v1:
time: 126 us; the launch traced here: 125 us
  starting transfers between devices  81.7 us (65%)
  waiting for transfers between devices  25.4 us (20%)
  matrix products  7.35 us (6%)
  local copies, waits for them, and re-layouts  6.28 us (5%)
  other arithmetic  4.06 us (3%)
    ppermute x2, starting transfers between devices, reduce(): total = lax.ppermute(total + far_p[:2 * height], 'layer', onward)  10 us
    ppermute x2, starting transfers between devices, reduce(): total = lax.ppermute(total + far_p[2 * height:4 * height], 'layer', onward)  10 us
    ppermute x2, starting transfers between devices, reduce(): total = lax.ppermute(near_p[:height], 'layer', onward)  8.07 us
    ppermute x2, starting transfers between devices, reduce(): total = lax.ppermute(total, 'layer', onward)  7.85 us
    all_to_all x1, starting transfers between devices, body(): lax.all_to_all(spread, 'col', split_axis=0, concat_axis=0, tiled=True)  7.7 us
    ppermute x1, starting transfers between devices, body(): in_both = lax.ppermute(pair_other, ('layer', 'row'), swap_both)  6.98 us
    dot_general x8, matrix products, dot(): lax.dot_general(a, b, (((0,), (0,)), ((), ())), precision=lax.Precision.H...  6.62 us
    all_to_all x1, waiting for transfers between devices, body(): lax.all_to_all(spread, 'col', split_axis=0, concat_axis=0, tiled=True)  6.52 us
  transfers between devices with their start and end apart: 19, of which 10 were waited for; matrix products, arithmetic and copies ran while one was open for 10% of the time, Pallas kernels for 0%

profile of v1, /device:TPU:1, one launch (start us, length us, event | category | flops | bytes accessed | tf_op | source)
XLA Modules:
  0.0 125.4 jit_solution(2690351178980558242)
XLA Ops:
  0.0 1.3 %constant_dynamic-slice_fusion.12 = (f32[64,2048]{1,0:T(8,128)S(1)}, f32[64,2048]{1,0:T(8,128)S(1)}) fusion(f32[64,4096]{1,0:T(8,128)} %param.3, s32[]{:T(128)S(6)} %select_n.187, s32[]{:T(128)S(6)} %select_n.186), kind=kLoop, calls=%fused_computation.94 | loop fusion | bytes 2097160 | tf_op jit(solution)/shard_map/dynamic_slice | solution.py:60
  1.3 5.2 %collective-permute-start.2 = (f32[64,2048]{1,0:T(8,128)S(1)}, f32[64,2048]{1,0:T(8,128)S(1)}, u32[]{:S(2)}, u32[]{:S(2)}) collective-permute-start(f32[64,2048]{1,0:T(8,128)S(1)} %get-tuple-element.7), channel_id=1, source_target_pairs={{8,0},{16,8},{24,16},{0,24},{9,1},{17,9},{25,17},{1,25},{10,2},{18... | collective-permute-start | bytes 1572872 | tf_op jit(solution)/shard_map/ppermute | solution.py:63
  6.5 1.9 %collective-permute-start.1 = (f32[64,2048]{1,0:T(8,128)S(1)}, f32[64,2048]{1,0:T(8,128)S(1)}, u32[]{:S(2)}, u32[]{:S(2)}) collective-permute-start(f32[64,2048]{1,0:T(8,128)S(1)} %get-tuple-element.7), channel_id=1, source_target_pairs={{0,8},{8,16},{16,24},{24,0},{1,9},{9,17},{17,25},{25,1},{2,10},{10... | collective-permute-start | bytes 1572872 | tf_op jit(solution)/shard_map/ppermute | solution.py:62
  8.5 3.6 %collective-permute-start.3 = (f32[64,2048]{1,0:T(8,128)S(1)}, f32[64,2048]{1,0:T(8,128)S(1)}, u32[]{:S(2)}, u32[]{:S(2)}) collective-permute-start(f32[64,2048]{1,0:T(8,128)S(1)} %get-tuple-element.8), channel_id=1, source_target_pairs={{0,16},{8,24},{16,0},{24,8},{1,17},{9,25},{17,1},{25,9},{2,18},{10... | collective-permute-start | bytes 1572872 | tf_op jit(solution)/shard_map/ppermute | solution.py:64
  12.2 0.7 convolution_bitcast_fusion
  13.0 5.8 %collective-permute-start = (f32[32,256]{1,0:T(8,128)S(1)}, f32[32,256]{1,0:T(8,128)S(1)}, u32[]{:S(2)}, u32[]{:S(2)}) collective-permute-start(f32[32,256]{1,0:T(8,128)S(1)} %get-tuple-element.36), channel_id=1, source_target_pairs={{0,32},{32,0},{64,96},{96,64},{128,160},{160,128},{192,224},{224,1... | collective-permute-start | bytes 98312 | tf_op jit(solution)/shard_map/ppermute | solution.py:57
  18.7 0.8 collective-permute-done
  19.6 0.8 broadcast_in_dim.22
  20.4 7.7 %all-to-all-start = ((f32[8,64,256]{2,1,0:T(8,128)}), f32[8,64,256]{2,1,0:T(8,128)}, u32[]{:S(2)}, u32[]{:S(2)}) async-start(f32[8,64,256]{2,1,0:T(8,128)} %broadcast_in_dim.22), calls=%async_computation | async-start | bytes 1048576 | tf_op jit(solution)/shard_map/all_to_all | solution.py:69
  28.1 4.4 %collective-permute-done.3 = f32[64,2048]{1,0:T(8,128)S(1)} collective-permute-done((f32[64,2048]{1,0:T(8,128)S(1)}, f32[64,2048]{1,0:T(8,128)S(1)}, u32[]{:S(2)}, u32[]{:S(2)}) %collective-permute-start.3) | collective-permute-done | bytes 524320 | tf_op jit(solution)/shard_map/ppermute | solution.py:64
  32.5 0.8 copy-done.3
  33.3 0.8 copy-done.1
  34.1 1.6 %pad_maximum_fusion = f32[256,2048]{1,0:T(8,128)} fusion(f32[64,2048]{1,0:T(8,128)S(1)} %collective-permute-done.3, f32[64,2048]{1,0:T(8,128)S(1)} %collective-permute-done.2, f32[64,2048]{1,0:T(8,128)S(1)} %collective-permute-done.1, f32[64,2048]{1,0:T(8,128)S(1)} %get-tuple-element.8), kind=kLoop, calls=%fused_computation.4 | loop fusion | flops 1572864 | bytes 4194304 | tf_op jit(solution)/shard_map/concatenate | solution.py:65
  35.7 3.8 %collective-permute-start.4 = (f32[256,2048]{1,0:T(8,128)}, f32[256,2048]{1,0:T(8,128)S(1)}, u32[]{:S(2)}, u32[]{:S(2)}) collective-permute-start(f32[256,2048]{1,0:T(8,128)} %pad_maximum_fusion), channel_id=1, source_target_pairs={{0,32},{32,0},{64,96},{96,64},{128,160},{160,128},{192,224},{224,1... | collective-permute-start | bytes 6291464 | tf_op jit(solution)/shard_map/ppermute | solution.py:66
  39.6 6.5 %all-to-all-done = f32[8,64,256]{2,1,0:T(8,128)} async-done(((f32[8,64,256]{2,1,0:T(8,128)}), f32[8,64,256]{2,1,0:T(8,128)}, u32[]{:S(2)}, u32[]{:S(2)}) %all-to-all-start) | async-done | bytes 524320 | tf_op jit(solution)/shard_map/all_to_all | solution.py:69
  46.2 1.0 slice.118
  47.1 1.2 slice.124
  48.5 3.4 %collective-permute-start.10 = (f32[2,256,96]{2,1,0:T(8,128)S(1)}, f32[2,256,96]{2,1,0:T(8,128)S(1)}, u32[]{:S(2)}, u32[]{:S(2)}) collective-permute-start(f32[2,256,96]{2,1,0:T(8,128)S(1)} %bitcast.43), channel_id=1, source_target_pairs={{0,8},{8,0},{16,24},{24,16},{1,9},{9,1},{17,25},{25,17},{2,10},{10... | collective-permute-start | bytes 589832 | tf_op jit(solution)/shard_map/ppermute | solution.py:82
  51.9 0.1 constant_dynamic-slice_fusion.11
  52.1 1.9 %collective-permute-start.13 = (f32[2,256,160]{2,1,0:T(8,128)S(1)}, f32[2,256,160]{2,1,0:T(8,128)S(1)}, u32[]{:S(2)}, u32[]{:S(2)}) collective-permute-start(f32[2,256,160]{2,1,0:T(8,128)S(1)} %bitcast.40), channel_id=1, source_target_pairs={{0,8},{8,0},{16,24},{24,16},{1,9},{9,1},{17,25},{25,17},{2,10},{10... | collective-permute-start | bytes 983048 | tf_op jit(solution)/shard_map/ppermute | solution.py:83
  54.2 3.7 %collective-permute-done.10 = f32[2,256,96]{2,1,0:T(8,128)S(1)} collective-permute-done((f32[2,256,96]{2,1,0:T(8,128)S(1)}, f32[2,256,96]{2,1,0:T(8,128)S(1)}, u32[]{:S(2)}, u32[]{:S(2)}) %collective-permute-start.10) | collective-permute-done | bytes 196640 | tf_op jit(solution)/shard_map/ppermute | solution.py:82
  57.9 0.8 fusion.38
  58.7 0.8 convolution_add_fusion.2
  59.6 5.1 %collective-permute-start.11 = (f32[32,2048]{1,0:T(8,128)S(1)}, f32[32,2048]{1,0:T(8,128)S(1)}, u32[]{:S(2)}, u32[]{:S(2)}) collective-permute-start(f32[32,2048]{1,0:T(8,128)S(1)} %slice.135), channel_id=1, source_target_pairs={{0,64},{64,128},{128,192},{192,256},{256,320},{320,384},{384,448},... | collective-permute-start | bytes 786440 | tf_op jit(solution)/shard_map/ppermute | solution.py:91
  64.7 0.8 fusion.59
  65.5 0.8 convolution_add_fusion.3
  66.4 3.0 %collective-permute-start.5 = (f32[32,2048]{1,0:T(8,128)S(1)}, f32[32,2048]{1,0:T(8,128)S(1)}, u32[]{:S(2)}, u32[]{:S(2)}) collective-permute-start(f32[32,2048]{1,0:T(8,128)S(1)} %slice.122), channel_id=1, source_target_pairs={{0,64},{64,128},{128,192},{192,256},{256,320},{320,384},{384,448},... | collective-permute-start | bytes 786440 | tf_op jit(solution)/shard_map/ppermute | solution.py:91
  69.4 0.8 fusion.36
  70.2 0.8 fusion.60
  71.0 0.9 convolution_add_fusion
  72.0 4.9 %collective-permute-start.12 = (f32[64,2048]{1,0:T(8,128)S(1)}, f32[64,2048]{1,0:T(8,128)S(1)}, u32[]{:S(2)}, u32[]{:S(2)}) collective-permute-start(f32[64,2048]{1,0:T(8,128)S(1)} %pad_maximum_fusion.2), channel_id=1, source_target_pairs={{0,64},{64,128},{128,192},{192,256},{256,320},{320,384},{384,448},... | collective-permute-start | bytes 1572872 | tf_op jit(solution)/shard_map/ppermute | solution.py:96
  77.0 3.0 %collective-permute-start.6 = (f32[64,2048]{1,0:T(8,128)S(1)}, f32[64,2048]{1,0:T(8,128)S(1)}, u32[]{:S(2)}, u32[]{:S(2)}) collective-permute-start(f32[64,2048]{1,0:T(8,128)S(1)} %pad_maximum_fusion.1), channel_id=1, source_target_pairs={{0,64},{64,128},{128,192},{192,256},{256,320},{320,384},{384,448},... | collective-permute-start | bytes 1572872 | tf_op jit(solution)/shard_map/ppermute | solution.py:96
  80.0 0.8 convolution_add_fusion.1
  80.8 2.1 %collective-permute-done.12 = f32[64,2048]{1,0:T(8,128)S(1)} collective-permute-done((f32[64,2048]{1,0:T(8,128)S(1)}, f32[64,2048]{1,0:T(8,128)S(1)}, u32[]{:S(2)}, u32[]{:S(2)}) %collective-permute-start.12) | collective-permute-done | bytes 524320 | tf_op jit(solution)/shard_map/ppermute | solution.py:96
  83.0 5.0 %collective-permute-start.14 = (f32[64,2048]{1,0:T(8,128)S(1)}, f32[64,2048]{1,0:T(8,128)S(1)}, u32[]{:S(2)}, u32[]{:S(2)}) collective-permute-start(f32[64,2048]{1,0:T(8,128)S(1)} %slice_add_fusion.1), channel_id=1, source_target_pairs={{0,64},{64,128},{128,192},{192,256},{256,320},{320,384},{384,448},... | collective-permute-start | bytes 1572872 | tf_op jit(solution)/shard_map/ppermute | solution.py:97
  88.1 0.5 collective-permute-done.6
  88.7 5.0 %collective-permute-start.7 = (f32[64,2048]{1,0:T(8,128)S(1)}, f32[64,2048]{1,0:T(8,128)S(1)}, u32[]{:S(2)}, u32[]{:S(2)}) collective-permute-start(f32[64,2048]{1,0:T(8,128)S(1)} %slice_add_fusion.3), channel_id=1, source_target_pairs={{0,64},{64,128},{128,192},{192,256},{256,320},{320,384},{384,448},... | collective-permute-start | bytes 1572872 | tf_op jit(solution)/shard_map/ppermute | solution.py:97
  93.7 0.5 collective-permute-done.14
  94.3 5.0 %collective-permute-start.15 = (f32[64,2048]{1,0:T(8,128)S(1)}, f32[64,2048]{1,0:T(8,128)S(1)}, u32[]{:S(2)}, u32[]{:S(2)}) collective-permute-start(f32[64,2048]{1,0:T(8,128)S(1)} %slice_add_fusion), channel_id=1, source_target_pairs={{0,64},{64,128},{128,192},{192,256},{256,320},{320,384},{384,448},... | collective-permute-start | bytes 1572872 | tf_op jit(solution)/shard_map/ppermute | solution.py:98
  99.3 0.5 collective-permute-done.7
  99.9 5.0 %collective-permute-start.8 = (f32[64,2048]{1,0:T(8,128)S(1)}, f32[64,2048]{1,0:T(8,128)S(1)}, u32[]{:S(2)}, u32[]{:S(2)}) collective-permute-start(f32[64,2048]{1,0:T(8,128)S(1)} %slice_add_fusion.2), channel_id=1, source_target_pairs={{0,64},{64,128},{128,192},{192,256},{256,320},{320,384},{384,448},... | collective-permute-start | bytes 1572872 | tf_op jit(solution)/shard_map/ppermute | solution.py:98
  104.9 0.5 collective-permute-done.15
  105.5 3.3 %collective-permute-start.16 = (f32[32,2048]{1,0:T(8,128)S(1)}, f32[32,2048]{1,0:T(8,128)S(1)}, u32[]{:S(2)}, u32[]{:S(2)}) collective-permute-start(f32[32,2048]{1,0:T(8,128)S(1)} %get-tuple-element.24), channel_id=1, source_target_pairs={{0,8},{8,0},{16,24},{24,16},{1,9},{9,1},{17,25},{25,17},{2,10},{10... | collective-permute-start | bytes 786440 | tf_op jit(solution)/shard_map/ppermute | solution.py:104
  108.8 7.0 %collective-permute-start.17 = (f32[32,2048]{1,0:T(8,128)S(1)}, f32[32,2048]{1,0:T(8,128)S(1)}, u32[]{:S(2)}, u32[]{:S(2)}) collective-permute-start(f32[32,2048]{1,0:T(8,128)S(1)} %get-tuple-element.23), channel_id=1, source_target_pairs={{0,40},{8,32},{16,56},{24,48},{32,8},{40,0},{48,24},{56,16},{64,10... | collective-permute-start | bytes 786440 | tf_op jit(solution)/shard_map/ppermute | solution.py:105
  115.8 2.0 %collective-permute-start.9 = (f32[32,2048]{1,0:T(8,128)S(1)}, f32[32,2048]{1,0:T(8,128)S(1)}, u32[]{:S(2)}, u32[]{:S(2)}) collective-permute-start(f32[32,2048]{1,0:T(8,128)S(1)} %slice.131), channel_id=1, source_target_pairs={{0,32},{32,0},{64,96},{96,64},{128,160},{160,128},{192,224},{224,1... | collective-permute-start | bytes 786440 | tf_op jit(solution)/shard_map/ppermute | solution.py:103
  117.9 5.7 %collective-permute-done.17 = f32[32,2048]{1,0:T(8,128)S(1)} collective-permute-done((f32[32,2048]{1,0:T(8,128)S(1)}, f32[32,2048]{1,0:T(8,128)S(1)}, u32[]{:S(2)}, u32[]{:S(2)}) %collective-permute-start.17) | collective-permute-done | bytes 262176 | tf_op jit(solution)/shard_map/ppermute | solution.py:105
  123.6 1.0 broadcast_select_fusion.1
  124.6 0.8 pad_maximum_fusion.3
  (46 shorter events, 0.9 us)
Async XLA Ops:
  0.0 12.2 %copy-start = (f32[512,32]{0,1:T(8,128)S(1)}, f32[512,32]{0,1:T(8,128)}, u32[]{:S(2)}) copy-start(f32[512,32]{0,1:T(8,128)} %param.2) | copy-start | bytes 196612
  1.3 31.2 %collective-permute-start.2 = (f32[64,2048]{1,0:T(8,128)S(1)}, f32[64,2048]{1,0:T(8,128)S(1)}, u32[]{:S(2)}, u32[]{:S(2)}) collective-permute-start(f32[64,2048]{1,0:T(8,128)S(1)} %get-tuple-element.7), channel_id=1, source_target_pairs={{8,0},{16,8},{24,16},{0,24},{9,1},{17,9},{25,17},{1,25},{10,2},{18... | collective-permute-start | bytes 1572872 | tf_op jit(solution)/shard_map/ppermute | solution.py:63
  6.5 26.0 %collective-permute-start.1 = (f32[64,2048]{1,0:T(8,128)S(1)}, f32[64,2048]{1,0:T(8,128)S(1)}, u32[]{:S(2)}, u32[]{:S(2)}) collective-permute-start(f32[64,2048]{1,0:T(8,128)S(1)} %get-tuple-element.7), channel_id=1, source_target_pairs={{0,8},{8,16},{16,24},{24,0},{1,9},{9,17},{17,25},{25,1},{2,10},{10... | collective-permute-start | bytes 1572872 | tf_op jit(solution)/shard_map/ppermute | solution.py:62
  8.5 24.0 %collective-permute-start.3 = (f32[64,2048]{1,0:T(8,128)S(1)}, f32[64,2048]{1,0:T(8,128)S(1)}, u32[]{:S(2)}, u32[]{:S(2)}) collective-permute-start(f32[64,2048]{1,0:T(8,128)S(1)} %get-tuple-element.8), channel_id=1, source_target_pairs={{0,16},{8,24},{16,0},{24,8},{1,17},{9,25},{17,1},{25,9},{2,18},{10... | collective-permute-start | bytes 1572872 | tf_op jit(solution)/shard_map/ppermute | solution.py:64
  13.0 6.6 %collective-permute-start = (f32[32,256]{1,0:T(8,128)S(1)}, f32[32,256]{1,0:T(8,128)S(1)}, u32[]{:S(2)}, u32[]{:S(2)}) collective-permute-start(f32[32,256]{1,0:T(8,128)S(1)} %get-tuple-element.36), channel_id=1, source_target_pairs={{0,32},{32,0},{64,96},{96,64},{128,160},{160,128},{192,224},{224,1... | collective-permute-start | bytes 98312 | tf_op jit(solution)/shard_map/ppermute | solution.py:57
  20.4 25.8 %all-to-all-start = ((f32[8,64,256]{2,1,0:T(8,128)}), f32[8,64,256]{2,1,0:T(8,128)}, u32[]{:S(2)}, u32[]{:S(2)}) async-start(f32[8,64,256]{2,1,0:T(8,128)} %broadcast_in_dim.22), calls=%async_computation | async-start | bytes 1048576 | tf_op jit(solution)/shard_map/all_to_all | solution.py:69
  32.5 0.8 copy-start.3
  33.3 0.8 copy-start.1
  35.7 22.2 %collective-permute-start.4 = (f32[256,2048]{1,0:T(8,128)}, f32[256,2048]{1,0:T(8,128)S(1)}, u32[]{:S(2)}, u32[]{:S(2)}) collective-permute-start(f32[256,2048]{1,0:T(8,128)} %pad_maximum_fusion), channel_id=1, source_target_pairs={{0,32},{32,0},{64,96},{96,64},{128,160},{160,128},{192,224},{224,1... | collective-permute-start | bytes 6291464 | tf_op jit(solution)/shard_map/ppermute | solution.py:66
  48.5 9.4 %collective-permute-start.10 = (f32[2,256,96]{2,1,0:T(8,128)S(1)}, f32[2,256,96]{2,1,0:T(8,128)S(1)}, u32[]{:S(2)}, u32[]{:S(2)}) collective-permute-start(f32[2,256,96]{2,1,0:T(8,128)S(1)} %bitcast.43), channel_id=1, source_target_pairs={{0,8},{8,0},{16,24},{24,16},{1,9},{9,1},{17,25},{25,17},{2,10},{10... | collective-permute-start | bytes 589832 | tf_op jit(solution)/shard_map/ppermute | solution.py:82
  52.1 17.2 %collective-permute-start.13 = (f32[2,256,160]{2,1,0:T(8,128)S(1)}, f32[2,256,160]{2,1,0:T(8,128)S(1)}, u32[]{:S(2)}, u32[]{:S(2)}) collective-permute-start(f32[2,256,160]{2,1,0:T(8,128)S(1)} %bitcast.40), channel_id=1, source_target_pairs={{0,8},{8,0},{16,24},{24,16},{1,9},{9,1},{17,25},{25,17},{2,10},{10... | collective-permute-start | bytes 983048 | tf_op jit(solution)/shard_map/ppermute | solution.py:83
  54.1 4.6 %copy-start.2 = (f32[64,2048]{1,0:T(8,128)S(1)}, f32[64,2048]{1,0:T(8,128)}, u32[]{:S(2)}) copy-start(f32[64,2048]{1,0:T(8,128)} %copy-done.1) | copy-start | bytes 1572868
  54.1 4.6 %copy-start.4 = (f32[64,2048]{1,0:T(8,128)S(1)}, f32[64,2048]{1,0:T(8,128)}, u32[]{:S(2)}) copy-start(f32[64,2048]{1,0:T(8,128)} %copy-done.3) | copy-start | bytes 1572868
  59.6 12.3 %collective-permute-start.11 = (f32[32,2048]{1,0:T(8,128)S(1)}, f32[32,2048]{1,0:T(8,128)S(1)}, u32[]{:S(2)}, u32[]{:S(2)}) collective-permute-start(f32[32,2048]{1,0:T(8,128)S(1)} %slice.135), channel_id=1, source_target_pairs={{0,64},{64,128},{128,192},{192,256},{256,320},{320,384},{384,448},... | collective-permute-start | bytes 786440 | tf_op jit(solution)/shard_map/ppermute | solution.py:91
  66.4 10.5 %collective-permute-start.5 = (f32[32,2048]{1,0:T(8,128)S(1)}, f32[32,2048]{1,0:T(8,128)S(1)}, u32[]{:S(2)}, u32[]{:S(2)}) collective-permute-start(f32[32,2048]{1,0:T(8,128)S(1)} %slice.122), channel_id=1, source_target_pairs={{0,64},{64,128},{128,192},{192,256},{256,320},{320,384},{384,448},... | collective-permute-start | bytes 786440 | tf_op jit(solution)/shard_map/ppermute | solution.py:91
  72.0 11.0 %collective-permute-start.12 = (f32[64,2048]{1,0:T(8,128)S(1)}, f32[64,2048]{1,0:T(8,128)S(1)}, u32[]{:S(2)}, u32[]{:S(2)}) collective-permute-start(f32[64,2048]{1,0:T(8,128)S(1)} %pad_maximum_fusion.2), channel_id=1, source_target_pairs={{0,64},{64,128},{128,192},{192,256},{256,320},{320,384},{384,448},... | collective-permute-start | bytes 1572872 | tf_op jit(solution)/shard_map/ppermute | solution.py:96
  77.0 11.6 %collective-permute-start.6 = (f32[64,2048]{1,0:T(8,128)S(1)}, f32[64,2048]{1,0:T(8,128)S(1)}, u32[]{:S(2)}, u32[]{:S(2)}) collective-permute-start(f32[64,2048]{1,0:T(8,128)S(1)} %pad_maximum_fusion.1), channel_id=1, source_target_pairs={{0,64},{64,128},{128,192},{192,256},{256,320},{320,384},{384,448},... | collective-permute-start | bytes 1572872 | tf_op jit(solution)/shard_map/ppermute | solution.py:96
  80.8 19.0 %copy-start.5 = (f32[160,2048]{1,0:T(8,128)}, f32[160,2048]{1,0:T(8,128)S(1)}, u32[]{:S(2)}) copy-start(f32[160,2048]{1,0:T(8,128)S(1)} %convolution_add_fusion.1) | copy-start | bytes 3932164
  83.0 11.2 %collective-permute-start.14 = (f32[64,2048]{1,0:T(8,128)S(1)}, f32[64,2048]{1,0:T(8,128)S(1)}, u32[]{:S(2)}, u32[]{:S(2)}) collective-permute-start(f32[64,2048]{1,0:T(8,128)S(1)} %slice_add_fusion.1), channel_id=1, source_target_pairs={{0,64},{64,128},{128,192},{192,256},{256,320},{320,384},{384,448},... | collective-permute-start | bytes 1572872 | tf_op jit(solution)/shard_map/ppermute | solution.py:97
  88.7 11.2 %collective-permute-start.7 = (f32[64,2048]{1,0:T(8,128)S(1)}, f32[64,2048]{1,0:T(8,128)S(1)}, u32[]{:S(2)}, u32[]{:S(2)}) collective-permute-start(f32[64,2048]{1,0:T(8,128)S(1)} %slice_add_fusion.3), channel_id=1, source_target_pairs={{0,64},{64,128},{128,192},{192,256},{256,320},{320,384},{384,448},... | collective-permute-start | bytes 1572872 | tf_op jit(solution)/shard_map/ppermute | solution.py:97
  94.3 11.2 %collective-permute-start.15 = (f32[64,2048]{1,0:T(8,128)S(1)}, f32[64,2048]{1,0:T(8,128)S(1)}, u32[]{:S(2)}, u32[]{:S(2)}) collective-permute-start(f32[64,2048]{1,0:T(8,128)S(1)} %slice_add_fusion), channel_id=1, source_target_pairs={{0,64},{64,128},{128,192},{192,256},{256,320},{320,384},{384,448},... | collective-permute-start | bytes 1572872 | tf_op jit(solution)/shard_map/ppermute | solution.py:98
  99.9 15.9 %collective-permute-start.8 = (f32[64,2048]{1,0:T(8,128)S(1)}, f32[64,2048]{1,0:T(8,128)S(1)}, u32[]{:S(2)}, u32[]{:S(2)}) collective-permute-start(f32[64,2048]{1,0:T(8,128)S(1)} %slice_add_fusion.2), channel_id=1, source_target_pairs={{0,64},{64,128},{128,192},{192,256},{256,320},{320,384},{384,448},... | collective-permute-start | bytes 1572872 | tf_op jit(solution)/shard_map/ppermute | solution.py:98
  105.5 12.4 %collective-permute-start.16 = (f32[32,2048]{1,0:T(8,128)S(1)}, f32[32,2048]{1,0:T(8,128)S(1)}, u32[]{:S(2)}, u32[]{:S(2)}) collective-permute-start(f32[32,2048]{1,0:T(8,128)S(1)} %get-tuple-element.24), channel_id=1, source_target_pairs={{0,8},{8,0},{16,24},{24,16},{1,9},{9,1},{17,25},{25,17},{2,10},{10... | collective-permute-start | bytes 786440 | tf_op jit(solution)/shard_map/ppermute | solution.py:104
  108.8 14.7 %collective-permute-start.17 = (f32[32,2048]{1,0:T(8,128)S(1)}, f32[32,2048]{1,0:T(8,128)S(1)}, u32[]{:S(2)}, u32[]{:S(2)}) collective-permute-start(f32[32,2048]{1,0:T(8,128)S(1)} %get-tuple-element.23), channel_id=1, source_target_pairs={{0,40},{8,32},{16,56},{24,48},{32,8},{40,0},{48,24},{56,16},{64,10... | collective-permute-start | bytes 786440 | tf_op jit(solution)/shard_map/ppermute | solution.py:105
  115.8 7.7 %collective-permute-start.9 = (f32[32,2048]{1,0:T(8,128)S(1)}, f32[32,2048]{1,0:T(8,128)S(1)}, u32[]{:S(2)}, u32[]{:S(2)}) collective-permute-start(f32[32,2048]{1,0:T(8,128)S(1)} %slice.131), channel_id=1, source_target_pairs={{0,32},{32,0},{64,96},{96,64},{128,160},{160,128},{192,224},{224,1... | collective-permute-start | bytes 786440 | tf_op jit(solution)/shard_map/ppermute | solution.py:103

commit v2 on v1

v2 whole, which is shorter than its diff:
```python
import jax
import jax.numpy as jnp
from jax import lax
from jax.sharding import PartitionSpec as P


def dot(a, b):
    return lax.dot_general(
        a,
        b,
        (((0,), (0,)), ((), ())),
        precision=lax.Precision.HIGH,
        preferred_element_type=jnp.float32,
    )


def body(left, right):
    layers, rows = lax.axis_size("layer"), lax.axis_size("row")
    cols = lax.axis_size("col")
    ys = layers // 2
    layer, x = lax.axis_index("layer"), lax.axis_index("row")
    y, c = layer // 2, layer % 2
    n = x % 2
    width = right.shape[1] // 2
    depth = left.shape[1]
    height = left.shape[0] // layers

    swap_core = [(i, i ^ 1) for i in range(layers)]
    swap_pair = [(i, i ^ 1) for i in range(rows)]
    onward = [(2 * i, 2 * ((i + 1) % ys)) for i in range(ys)]
    onward += [(2 * i + 1, 2 * ((i - 1) % ys) + 1) for i in range(ys)]
    onward_cross = [(i, j ^ 1) for i, j in onward]

    def joint(pairs):
        return [(i * rows + k, j * rows + (k ^ 1)) for i, j in pairs for k in range(rows)]


    def block_of(slot, core):
        away = jnp.where(slot == 0, 4, jnp.where(slot == 7, 0, 3 - (slot - 1) // 2))
        half = jnp.where((slot == 0) | (slot == 7), core, core ^ ((slot + 1) % 2))
        return ((y + (1 - 2 * core) * away) % ys) * 2 + half

    slots = 8
    quarter = slots * height // 2
    lane = lax.broadcasted_iota(jnp.int32, (left.shape[0], 4 * quarter), 1)
    source = lax.broadcasted_iota(jnp.int32, (left.shape[0], 4 * quarter), 0)
    core = jnp.where((lane // quarter) % 2 == 0, c, 1 - c)
    slot = (lane // (2 * quarter)) * (slots // 2) + (lane % quarter) // height
    wanted = block_of(slot, core) * height + lane % height
    picked = lax.dot_general(
        left,
        (source == wanted).astype(jnp.float32),
        (((0,), (0,)), ((), ())),
        precision=lax.Precision.HIGHEST,
    )

    keep = lax.dynamic_slice_in_dim(right, n * width, width, 1)
    give = lax.dynamic_slice_in_dim(right, (1 - n) * width, width, 1)
    step = [(i, (i + 1) % rows) for i in range(rows)]
    from_low = lax.ppermute(give, "row", step)
    from_high = lax.ppermute(give, "row", [(j, i) for i, j in step])
    from_far = lax.ppermute(keep, "row", [(i, (i + 2) % rows) for i in range(rows)])
    own_b = jnp.concatenate([keep, from_far, from_high, from_low], 0)

    spread = jnp.broadcast_to(picked[None], (cols,) + picked.shape)
    full = lax.all_to_all(spread, "col", split_axis=0, concat_axis=0, tiled=True)
    full = full.reshape(rows, cols // rows * depth, 4 * quarter)

    def ordered(part, at):
        order = [at, at + 2, at + 1, at - 1]
        return jnp.concatenate(
            [lax.dynamic_index_in_dim(part, i % rows, 0, keepdims=False) for i in order],
            0,
        )

    near_a, far_a = full[..., : 2 * quarter], full[..., 2 * quarter :]
    near_pair = lax.ppermute(ordered(near_a, x ^ 1), "row", swap_pair)
    far_pair = lax.ppermute(ordered(far_a, x ^ 1), "row", swap_pair)
    near_a, far_a = ordered(near_a, x), ordered(far_a, x)

    def product(a):
        part = dot(a, own_b)
        other = part[quarter:]
        return part[:quarter] + lax.ppermute(other, "layer", swap_core)

    def reduce(near, far):
        near_p = product(near)
        total = lax.ppermute(near_p[:height], "layer", onward)
        total = jnp.concatenate(
            [near_p[height : 2 * height] + total, near_p[2 * height : 3 * height]], 0
        )
        far_p = product(far)
        total = lax.ppermute(total, "layer", onward)
        total = jnp.concatenate(
            [
                total[:height] + near_p[3 * height :],
                total[height:] + far_p[:height],
            ],
            0,
        )
        total = lax.ppermute(total, "layer", onward)
        total = total + far_p[height : 3 * height]
        return total[:height], total[height:], far_p[3 * height :]

    same, cross, here = reduce(near_a, far_a)
    here = here + lax.ppermute(same, "layer", onward)
    here = here + lax.ppermute(cross, "layer", onward_cross)
    same, cross, there = reduce(near_pair, far_pair)
    there = lax.ppermute(there, "row", swap_pair)
    there = there + lax.ppermute(same, ("layer", "row"), joint(onward))
    there = there + lax.ppermute(cross, ("layer", "row"), joint(onward_cross))
    return jnp.concatenate(
        [jnp.where(n == 0, here, there), jnp.where(n == 0, there, here)], 1
    )


def solution(mesh):
    in_specs = (P("row", ("layer", "col")), P(("layer", "row"), "col"))
    out_specs = P(("row", "layer"), "col")
    return jax.shard_map(
        body, mesh=mesh, in_specs=in_specs, out_specs=out_specs, check_vma=False
    )
```

time: 126 us -> 126 us (level)
  waiting for transfers between devices: 25.4 us -> 33.1 us
  local copies, waits for them, and re-layouts: 6.28 us -> 2.28 us
  matrix products: 7.35 us -> 5.15 us
  other arithmetic: 4.06 us -> 2.72 us
    ppermute x11, starting transfers between devices: 47.3 us -> 34.3 us  [the longest x4 11.3 us: product(): return part[:quarter] + lax.ppermute(other, 'layer', swap_core)]
    ppermute x2 -> x4, starting transfers between devices: 7.85 us -> 18.1 us  [reduce(): total = lax.ppermute(total, 'layer', onward)]
    ppermute x1, waiting for transfers between devices: 4.41 us -> 9.89 us  [body(): lax.ppermute(keep, 'row', [(i, (i + 2) % rows) for i in range(rows)])]
    all_to_all x1, starting transfers between devices: 7.7 us -> 10.9 us  [body(): lax.all_to_all(spread, 'col', split_axis=0, concat_axis=0, tiled=True)]
    dot_general x8 -> x4, matrix products: 6.62 us -> 4.42 us  [dot(): lax.dot_general(a, b, (((0,), (0,)), ((), ())), precision=lax.Precision.H...]
    slice x6 -> x7, local copies, waits for them, and re-layouts: 2.29 us -> 0.45 us  [the longest x4 0.34 us: product(): other = part[quarter:]]
    ppermute x1, starting transfers between devices: 5.2 us -> 3.38 us  [body(): from_high = lax.ppermute(give, 'row', [(j, i) for i, j in step])]
    concatenate x4 -> x6, other arithmetic: 1.67 us -> 0.18 us  [the longest x2 0.07 us: reduce(): jnp.concatenate([near_p[height:2 * height] + total, near_p[2 * height:3 *...]
  transfers between devices with their start and end apart: 19 -> 21, of which waited for: 10 -> 8; matrix products, arithmetic and copies ran while one was open for 10% -> 5% of each run, Pallas kernels for 0% -> 0%
where the time goes in v2:
time: 126 us; the launch traced here: 125 us
  starting transfers between devices  81.3 us (65%)
  waiting for transfers between devices  33.1 us (26%)
  matrix products  5.15 us (4%)
  other arithmetic  2.72 us (2%)
  local copies, waits for them, and re-layouts  2.28 us (2%)
    ppermute x4, starting transfers between devices, reduce(): total = lax.ppermute(total, 'layer', onward)  18.1 us
    ppermute x4, starting transfers between devices, product(): return part[:quarter] + lax.ppermute(other, 'layer', swap_core)  11.3 us
    all_to_all x1, starting transfers between devices, body(): lax.all_to_all(spread, 'col', split_axis=0, concat_axis=0, tiled=True)  10.9 us
    ppermute x1, waiting for transfers between devices, body(): lax.ppermute(keep, 'row', [(i, (i + 2) % rows) for i in range(rows)])  9.89 us
    ppermute x2, starting transfers between devices, reduce(): total = lax.ppermute(near_p[:height], 'layer', onward)  8.07 us
    all_to_all x1, waiting for transfers between devices, body(): lax.all_to_all(spread, 'col', split_axis=0, concat_axis=0, tiled=True)  7.75 us
    ppermute x1, waiting for transfers between devices, body(): there = there + lax.ppermute(cross, ('layer', 'row'), joint(onward_cross))  4.6 us
    ppermute x1, waiting for transfers between devices, body(): there = there + lax.ppermute(same, ('layer', 'row'), joint(onward))  4.57 us
  transfers between devices with their start and end apart: 21, of which 8 were waited for; matrix products, arithmetic and copies ran while one was open for 5% of the time, Pallas kernels for 0%

profile of v2, /device:TPU:1, one launch (start us, length us, event | category | flops | bytes accessed | tf_op | source)
XLA Modules:
  0.0 125.2 jit_solution(12848548645548323903)
XLA Ops:
  0.1 0.7 copy-done
  0.8 0.7 convolution_bitcast_fusion
  1.6 0.9 broadcast_in_dim.19
  2.4 10.9 %all-to-all-start = ((f32[8,32,512]{2,1,0:T(8,128)}), f32[8,32,512]{2,1,0:T(8,128)S(1)}, u32[]{:S(2)}, u32[]{:S(2)}) async-start(f32[8,32,512]{2,1,0:T(8,128)} %broadcast_in_dim.19), calls=%async_computation | async-start | bytes 1048576 | tf_op jit(solution)/shard_map/all_to_all | solution.py:66
  13.3 0.1 constant_dynamic-slice_fusion.1
  13.4 3.1 %collective-permute-start.2 = (f32[64,2048]{1,0:T(8,128)S(1)}, f32[64,2048]{1,0:T(8,128)S(1)}, u32[]{:S(2)}, u32[]{:S(2)}) collective-permute-start(f32[64,2048]{1,0:T(8,128)S(1)} %get-tuple-element.14), channel_id=1, source_target_pairs={{0,8},{8,16},{16,24},{24,0},{1,9},{9,17},{17,25},{25,1},{2,10},{10... | collective-permute-start | bytes 1572872 | tf_op jit(solution)/shard_map/ppermute | solution.py:60
  16.5 3.4 %collective-permute-start.1 = (f32[64,2048]{1,0:T(8,128)S(1)}, f32[64,2048]{1,0:T(8,128)S(1)}, u32[]{:S(2)}, u32[]{:S(2)}) collective-permute-start(f32[64,2048]{1,0:T(8,128)S(1)} %get-tuple-element.14), channel_id=1, source_target_pairs={{8,0},{16,8},{24,16},{0,24},{9,1},{17,9},{25,17},{1,25},{10,2},{18... | collective-permute-start | bytes 1572872 | tf_op jit(solution)/shard_map/ppermute | solution.py:61
  19.9 3.4 %collective-permute-start = (f32[64,2048]{1,0:T(8,128)S(1)}, f32[64,2048]{1,0:T(8,128)S(1)}, u32[]{:S(2)}, u32[]{:S(2)}) collective-permute-start(f32[64,2048]{1,0:T(8,128)S(1)} %get-tuple-element.13), channel_id=1, source_target_pairs={{0,16},{8,24},{16,0},{24,8},{1,17},{9,25},{17,1},{25,9},{2,18},{10... | collective-permute-start | bytes 1572872 | tf_op jit(solution)/shard_map/ppermute | solution.py:62
  23.5 7.7 %all-to-all-done = f32[8,32,512]{2,1,0:T(8,128)S(1)} async-done(((f32[8,32,512]{2,1,0:T(8,128)}), f32[8,32,512]{2,1,0:T(8,128)S(1)}, u32[]{:S(2)}, u32[]{:S(2)}) %all-to-all-start) | async-done | bytes 524320 | tf_op jit(solution)/shard_map/all_to_all | solution.py:66
  31.4 9.9 %collective-permute-done = f32[64,2048]{1,0:T(8,128)S(1)} collective-permute-done((f32[64,2048]{1,0:T(8,128)S(1)}, f32[64,2048]{1,0:T(8,128)S(1)}, u32[]{:S(2)}, u32[]{:S(2)}) %collective-permute-start) | collective-permute-done | bytes 524320 | tf_op jit(solution)/shard_map/ppermute | solution.py:62
  41.3 1.1 fusion.59
  42.4 0.1 slice.134
  42.5 3.9 %collective-permute-start.4 = (f32[128,2048]{1,0:T(8,128)S(1)}, f32[128,2048]{1,0:T(8,128)S(1)}, u32[]{:S(2)}, u32[]{:S(2)}) collective-permute-start(f32[128,2048]{1,0:T(8,128)S(1)} %slice.134), channel_id=1, source_target_pairs={{0,32},{32,0},{64,96},{96,64},{128,160},{160,128},{192,224},{224,1... | collective-permute-start | bytes 3145736 | tf_op jit(solution)/shard_map/ppermute | solution.py:84
  46.5 4.5 %collective-permute-start.10 = (f32[256,256]{1,0:T(8,128)S(1)}, f32[256,256]{1,0:T(8,128)S(1)}, u32[]{:S(2)}, u32[]{:S(2)}) collective-permute-start(f32[256,256]{1,0:T(8,128)S(1)} %pad_maximum_fusion.6), channel_id=1, source_target_pairs={{0,8},{8,0},{16,24},{24,16},{1,9},{9,1},{17,25},{25,17},{2,10},{10... | collective-permute-start | bytes 786440 | tf_op jit(solution)/shard_map/ppermute | solution.py:78
  51.0 1.9 %collective-permute-start.13 = (f32[256,256]{1,0:T(8,128)S(1)}, f32[256,256]{1,0:T(8,128)S(1)}, u32[]{:S(2)}, u32[]{:S(2)}) collective-permute-start(f32[256,256]{1,0:T(8,128)S(1)} %pad_maximum_fusion.7), channel_id=1, source_target_pairs={{0,8},{8,0},{16,24},{24,16},{1,9},{9,1},{17,25},{25,17},{2,10},{10... | collective-permute-start | bytes 786440 | tf_op jit(solution)/shard_map/ppermute | solution.py:77
  52.9 1.1 fusion.51
  54.0 0.1 slice.130
  54.1 2.2 %collective-permute-start.3 = (f32[128,2048]{1,0:T(8,128)S(1)}, f32[128,2048]{1,0:T(8,128)S(1)}, u32[]{:S(2)}, u32[]{:S(2)}) collective-permute-start(f32[128,2048]{1,0:T(8,128)S(1)} %slice.130), channel_id=1, source_target_pairs={{0,32},{32,0},{64,96},{96,64},{128,160},{160,128},{192,224},{224,1... | collective-permute-start | bytes 3145736 | tf_op jit(solution)/shard_map/ppermute | solution.py:84
  56.3 1.3 %collective-permute-done.10 = f32[256,256]{1,0:T(8,128)S(1)} collective-permute-done((f32[256,256]{1,0:T(8,128)S(1)}, f32[256,256]{1,0:T(8,128)S(1)}, u32[]{:S(2)}, u32[]{:S(2)}) %collective-permute-start.10) | collective-permute-done | bytes 262176 | tf_op jit(solution)/shard_map/ppermute | solution.py:78
  57.6 1.1 fusion.93
  58.7 0.1 slice.146
  58.8 2.7 %collective-permute-start.11 = (f32[128,2048]{1,0:T(8,128)S(1)}, f32[128,2048]{1,0:T(8,128)S(1)}, u32[]{:S(2)}, u32[]{:S(2)}) collective-permute-start(f32[128,2048]{1,0:T(8,128)S(1)} %slice.146), channel_id=1, source_target_pairs={{0,32},{32,0},{64,96},{96,64},{128,160},{160,128},{192,224},{224,1... | collective-permute-start | bytes 3145736 | tf_op jit(solution)/shard_map/ppermute | solution.py:84
  61.5 1.7 %collective-permute-done.13 = f32[256,256]{1,0:T(8,128)S(1)} collective-permute-done((f32[256,256]{1,0:T(8,128)S(1)}, f32[256,256]{1,0:T(8,128)S(1)}, u32[]{:S(2)}, u32[]{:S(2)}) %collective-permute-start.13) | collective-permute-done | bytes 262176 | tf_op jit(solution)/shard_map/ppermute | solution.py:77
  63.2 1.1 fusion.92
  64.4 2.5 %collective-permute-start.14 = (f32[128,2048]{1,0:T(8,128)S(1)}, f32[128,2048]{1,0:T(8,128)S(1)}, u32[]{:S(2)}, u32[]{:S(2)}) collective-permute-start(f32[128,2048]{1,0:T(8,128)S(1)} %slice.149), channel_id=1, source_target_pairs={{0,32},{32,0},{64,96},{96,64},{128,160},{160,128},{192,224},{224,1... | collective-permute-start | bytes 3145736 | tf_op jit(solution)/shard_map/ppermute | solution.py:84
  66.9 0.1 slice_add_fusion.2
  67.1 5.1 %collective-permute-start.5 = (f32[32,2048]{1,0:T(8,128)S(1)}, f32[32,2048]{1,0:T(8,128)S(1)}, u32[]{:S(2)}, u32[]{:S(2)}) collective-permute-start(f32[32,2048]{1,0:T(8,128)S(1)} %slice.136), channel_id=1, source_target_pairs={{0,64},{64,128},{128,192},{192,256},{256,320},{320,384},{384,448},... | collective-permute-start | bytes 786440 | tf_op jit(solution)/shard_map/ppermute | solution.py:88
  72.2 0.1 slice_add_fusion.3
  72.3 0.1 slice_add_fusion
  72.5 3.0 %collective-permute-start.15 = (f32[32,2048]{1,0:T(8,128)S(1)}, f32[32,2048]{1,0:T(8,128)S(1)}, u32[]{:S(2)}, u32[]{:S(2)}) collective-permute-start(f32[32,2048]{1,0:T(8,128)S(1)} %slice.151), channel_id=1, source_target_pairs={{0,64},{64,128},{128,192},{192,256},{256,320},{320,384},{384,448},... | collective-permute-start | bytes 786440 | tf_op jit(solution)/shard_map/ppermute | solution.py:88
  75.6 5.0 %collective-permute-start.6 = (f32[64,2048]{1,0:T(8,128)S(1)}, f32[64,2048]{1,0:T(8,128)S(1)}, u32[]{:S(2)}, u32[]{:S(2)}) collective-permute-start(f32[64,2048]{1,0:T(8,128)S(1)} %pad_maximum_fusion.1), channel_id=1, source_target_pairs={{0,64},{64,128},{128,192},{192,256},{256,320},{320,384},{384,448},... | collective-permute-start | bytes 1572872 | tf_op jit(solution)/shard_map/ppermute | solution.py:93
  80.6 0.1 slice_add_fusion.1
  80.9 3.0 %collective-permute-start.16 = (f32[64,2048]{1,0:T(8,128)S(1)}, f32[64,2048]{1,0:T(8,128)S(1)}, u32[]{:S(2)}, u32[]{:S(2)}) collective-permute-start(f32[64,2048]{1,0:T(8,128)S(1)} %pad_maximum_fusion.3), channel_id=1, source_target_pairs={{0,64},{64,128},{128,192},{192,256},{256,320},{320,384},{384,448},... | collective-permute-start | bytes 1572872 | tf_op jit(solution)/shard_map/ppermute | solution.py:93
  83.9 2.8 %collective-permute-done.6 = f32[64,2048]{1,0:T(8,128)S(1)} collective-permute-done((f32[64,2048]{1,0:T(8,128)S(1)}, f32[64,2048]{1,0:T(8,128)S(1)}, u32[]{:S(2)}, u32[]{:S(2)}) %collective-permute-start.6) | collective-permute-done | bytes 524320 | tf_op jit(solution)/shard_map/ppermute | solution.py:93
  86.8 5.0 %collective-permute-start.7 = (f32[64,2048]{1,0:T(8,128)S(1)}, f32[64,2048]{1,0:T(8,128)S(1)}, u32[]{:S(2)}, u32[]{:S(2)}) collective-permute-start(f32[64,2048]{1,0:T(8,128)S(1)} %pad_maximum_fusion.2), channel_id=1, source_target_pairs={{0,64},{64,128},{128,192},{192,256},{256,320},{320,384},{384,448},... | collective-permute-start | bytes 1572872 | tf_op jit(solution)/shard_map/ppermute | solution.py:101
  91.9 0.5 collective-permute-done.16
  92.4 0.8 fusion.94
  93.2 5.0 %collective-permute-start.17 = (f32[64,2048]{1,0:T(8,128)S(1)}, f32[64,2048]{1,0:T(8,128)S(1)}, u32[]{:S(2)}, u32[]{:S(2)}) collective-permute-start(f32[64,2048]{1,0:T(8,128)S(1)} %pad_maximum_fusion.4), channel_id=1, source_target_pairs={{0,64},{64,128},{128,192},{192,256},{256,320},{320,384},{384,448},... | collective-permute-start | bytes 1572872 | tf_op jit(solution)/shard_map/ppermute | solution.py:101
  98.2 3.4 %collective-permute-start.12 = (f32[32,2048]{1,0:T(8,128)}, f32[32,2048]{1,0:T(8,128)S(1)}, u32[]{:S(2)}, u32[]{:S(2)}) collective-permute-start(f32[32,2048]{1,0:T(8,128)} %get-tuple-element.9), channel_id=1, source_target_pairs={{0,8},{8,0},{16,24},{24,16},{1,9},{9,1},{17,25},{25,17},{2,10},{10... | collective-permute-start | bytes 786440 | tf_op jit(solution)/shard_map/ppermute | solution.py:109
  101.7 4.4 %collective-permute-start.9 = (f32[32,2048]{1,0:T(8,128)S(1)}, f32[32,2048]{1,0:T(8,128)S(1)}, u32[]{:S(2)}, u32[]{:S(2)}) collective-permute-start(f32[32,2048]{1,0:T(8,128)S(1)} %get-tuple-element.17), channel_id=1, source_target_pairs={{0,96},{64,160},{128,224},{192,288},{256,352},{320,416},{384,480},... | collective-permute-start | bytes 786440 | tf_op jit(solution)/shard_map/ppermute | solution.py:107
  106.1 1.9 %collective-permute-start.8 = (f32[32,2048]{1,0:T(8,128)S(1)}, f32[32,2048]{1,0:T(8,128)S(1)}, u32[]{:S(2)}, u32[]{:S(2)}) collective-permute-start(f32[32,2048]{1,0:T(8,128)S(1)} %get-tuple-element.16), channel_id=1, source_target_pairs={{0,64},{64,128},{128,192},{192,256},{256,320},{320,384},{384,448},... | collective-permute-start | bytes 786440 | tf_op jit(solution)/shard_map/ppermute | solution.py:106
  108.0 0.1 slice_add_fusion.4
  108.2 3.4 %collective-permute-start.19 = (f32[32,2048]{1,0:T(8,128)S(1)}, f32[32,2048]{1,0:T(8,128)S(1)}, u32[]{:S(2)}, u32[]{:S(2)}) collective-permute-start(f32[32,2048]{1,0:T(8,128)S(1)} %get-tuple-element.21), channel_id=1, source_target_pairs={{0,104},{8,96},{16,120},{24,112},{64,168},{72,160},{80,184},{88,17... | collective-permute-start | bytes 786440 | tf_op jit(solution)/shard_map/ppermute | solution.py:111
  111.6 3.5 %collective-permute-start.18 = (f32[32,2048]{1,0:T(8,128)S(1)}, f32[32,2048]{1,0:T(8,128)S(1)}, u32[]{:S(2)}, u32[]{:S(2)}) collective-permute-start(f32[32,2048]{1,0:T(8,128)S(1)} %get-tuple-element.20), channel_id=1, source_target_pairs={{0,72},{8,64},{16,88},{24,80},{64,136},{72,128},{80,152},{88,144},... | collective-permute-start | bytes 786440 | tf_op jit(solution)/shard_map/ppermute | solution.py:110
  115.1 4.6 %collective-permute-done.19 = f32[32,2048]{1,0:T(8,128)S(1)} collective-permute-done((f32[32,2048]{1,0:T(8,128)S(1)}, f32[32,2048]{1,0:T(8,128)S(1)}, u32[]{:S(2)}, u32[]{:S(2)}) %collective-permute-start.19) | collective-permute-done | bytes 262176 | tf_op jit(solution)/shard_map/ppermute | solution.py:111
  119.8 4.6 %collective-permute-done.18 = f32[32,2048]{1,0:T(8,128)S(1)} collective-permute-done((f32[32,2048]{1,0:T(8,128)S(1)}, f32[32,2048]{1,0:T(8,128)S(1)}, u32[]{:S(2)}, u32[]{:S(2)}) %collective-permute-start.18) | collective-permute-done | bytes 262176 | tf_op jit(solution)/shard_map/ppermute | solution.py:110
  124.3 0.1 broadcast_select_fusion.1
  124.4 0.8 pad_maximum_fusion.5
  (40 shorter events, 0.8 us)
Async XLA Ops:
  0.0 0.8 copy-start
  1.6 11.7 %copy-start.1 = (f32[64,4096]{1,0:T(8,128)S(1)}, f32[64,4096]{1,0:T(8,128)}, u32[]{:S(2)}) copy-start(f32[64,4096]{1,0:T(8,128)} %param.3) | copy-start | bytes 3145732
  2.4 28.8 %all-to-all-start = ((f32[8,32,512]{2,1,0:T(8,128)}), f32[8,32,512]{2,1,0:T(8,128)S(1)}, u32[]{:S(2)}, u32[]{:S(2)}) async-start(f32[8,32,512]{2,1,0:T(8,128)} %broadcast_in_dim.19), calls=%async_computation | async-start | bytes 1048576 | tf_op jit(solution)/shard_map/all_to_all | solution.py:66
  13.4 17.9 %collective-permute-start.2 = (f32[64,2048]{1,0:T(8,128)S(1)}, f32[64,2048]{1,0:T(8,128)S(1)}, u32[]{:S(2)}, u32[]{:S(2)}) collective-permute-start(f32[64,2048]{1,0:T(8,128)S(1)} %get-tuple-element.14), channel_id=1, source_target_pairs={{0,8},{8,16},{16,24},{24,0},{1,9},{9,17},{17,25},{25,1},{2,10},{10... | collective-permute-start | bytes 1572872 | tf_op jit(solution)/shard_map/ppermute | solution.py:60
  16.5 14.8 %collective-permute-start.1 = (f32[64,2048]{1,0:T(8,128)S(1)}, f32[64,2048]{1,0:T(8,128)S(1)}, u32[]{:S(2)}, u32[]{:S(2)}) collective-permute-start(f32[64,2048]{1,0:T(8,128)S(1)} %get-tuple-element.14), channel_id=1, source_target_pairs={{8,0},{16,8},{24,16},{0,24},{9,1},{17,9},{25,17},{1,25},{10,2},{18... | collective-permute-start | bytes 1572872 | tf_op jit(solution)/shard_map/ppermute | solution.py:61
  19.9 21.3 %collective-permute-start = (f32[64,2048]{1,0:T(8,128)S(1)}, f32[64,2048]{1,0:T(8,128)S(1)}, u32[]{:S(2)}, u32[]{:S(2)}) collective-permute-start(f32[64,2048]{1,0:T(8,128)S(1)} %get-tuple-element.13), channel_id=1, source_target_pairs={{0,16},{8,24},{16,0},{24,8},{1,17},{9,25},{17,1},{25,9},{2,18},{10... | collective-permute-start | bytes 1572872 | tf_op jit(solution)/shard_map/ppermute | solution.py:62
  42.5 24.5 %collective-permute-start.4 = (f32[128,2048]{1,0:T(8,128)S(1)}, f32[128,2048]{1,0:T(8,128)S(1)}, u32[]{:S(2)}, u32[]{:S(2)}) collective-permute-start(f32[128,2048]{1,0:T(8,128)S(1)} %slice.134), channel_id=1, source_target_pairs={{0,32},{32,0},{64,96},{96,64},{128,160},{160,128},{192,224},{224,1... | collective-permute-start | bytes 3145736 | tf_op jit(solution)/shard_map/ppermute | solution.py:84
  46.5 11.1 %collective-permute-start.10 = (f32[256,256]{1,0:T(8,128)S(1)}, f32[256,256]{1,0:T(8,128)S(1)}, u32[]{:S(2)}, u32[]{:S(2)}) collective-permute-start(f32[256,256]{1,0:T(8,128)S(1)} %pad_maximum_fusion.6), channel_id=1, source_target_pairs={{0,8},{8,0},{16,24},{24,16},{1,9},{9,1},{17,25},{25,17},{2,10},{10... | collective-permute-start | bytes 786440 | tf_op jit(solution)/shard_map/ppermute | solution.py:78
  51.0 12.2 %collective-permute-start.13 = (f32[256,256]{1,0:T(8,128)S(1)}, f32[256,256]{1,0:T(8,128)S(1)}, u32[]{:S(2)}, u32[]{:S(2)}) collective-permute-start(f32[256,256]{1,0:T(8,128)S(1)} %pad_maximum_fusion.7), channel_id=1, source_target_pairs={{0,8},{8,0},{16,24},{24,16},{1,9},{9,1},{17,25},{25,17},{2,10},{10... | collective-permute-start | bytes 786440 | tf_op jit(solution)/shard_map/ppermute | solution.py:77
  54.1 18.1 %collective-permute-start.3 = (f32[128,2048]{1,0:T(8,128)S(1)}, f32[128,2048]{1,0:T(8,128)S(1)}, u32[]{:S(2)}, u32[]{:S(2)}) collective-permute-start(f32[128,2048]{1,0:T(8,128)S(1)} %slice.130), channel_id=1, source_target_pairs={{0,32},{32,0},{64,96},{96,64},{128,160},{160,128},{192,224},{224,1... | collective-permute-start | bytes 3145736 | tf_op jit(solution)/shard_map/ppermute | solution.py:84
  58.8 21.8 %collective-permute-start.11 = (f32[128,2048]{1,0:T(8,128)S(1)}, f32[128,2048]{1,0:T(8,128)S(1)}, u32[]{:S(2)}, u32[]{:S(2)}) collective-permute-start(f32[128,2048]{1,0:T(8,128)S(1)} %slice.146), channel_id=1, source_target_pairs={{0,32},{32,0},{64,96},{96,64},{128,160},{160,128},{192,224},{224,1... | collective-permute-start | bytes 3145736 | tf_op jit(solution)/shard_map/ppermute | solution.py:84
  64.4 7.9 %collective-permute-start.14 = (f32[128,2048]{1,0:T(8,128)S(1)}, f32[128,2048]{1,0:T(8,128)S(1)}, u32[]{:S(2)}, u32[]{:S(2)}) collective-permute-start(f32[128,2048]{1,0:T(8,128)S(1)} %slice.149), channel_id=1, source_target_pairs={{0,32},{32,0},{64,96},{96,64},{128,160},{160,128},{192,224},{224,1... | collective-permute-start | bytes 3145736 | tf_op jit(solution)/shard_map/ppermute | solution.py:84
  67.1 8.4 %collective-permute-start.5 = (f32[32,2048]{1,0:T(8,128)S(1)}, f32[32,2048]{1,0:T(8,128)S(1)}, u32[]{:S(2)}, u32[]{:S(2)}) collective-permute-start(f32[32,2048]{1,0:T(8,128)S(1)} %slice.136), channel_id=1, source_target_pairs={{0,64},{64,128},{128,192},{192,256},{256,320},{320,384},{384,448},... | collective-permute-start | bytes 786440 | tf_op jit(solution)/shard_map/ppermute | solution.py:88
  72.5 8.2 %collective-permute-start.15 = (f32[32,2048]{1,0:T(8,128)S(1)}, f32[32,2048]{1,0:T(8,128)S(1)}, u32[]{:S(2)}, u32[]{:S(2)}) collective-permute-start(f32[32,2048]{1,0:T(8,128)S(1)} %slice.151), channel_id=1, source_target_pairs={{0,64},{64,128},{128,192},{192,256},{256,320},{320,384},{384,448},... | collective-permute-start | bytes 786440 | tf_op jit(solution)/shard_map/ppermute | solution.py:88
  75.6 11.1 %collective-permute-start.6 = (f32[64,2048]{1,0:T(8,128)S(1)}, f32[64,2048]{1,0:T(8,128)S(1)}, u32[]{:S(2)}, u32[]{:S(2)}) collective-permute-start(f32[64,2048]{1,0:T(8,128)S(1)} %pad_maximum_fusion.1), channel_id=1, source_target_pairs={{0,64},{64,128},{128,192},{192,256},{256,320},{320,384},{384,448},... | collective-permute-start | bytes 1572872 | tf_op jit(solution)/shard_map/ppermute | solution.py:93
  80.9 11.5 %collective-permute-start.16 = (f32[64,2048]{1,0:T(8,128)S(1)}, f32[64,2048]{1,0:T(8,128)S(1)}, u32[]{:S(2)}, u32[]{:S(2)}) collective-permute-start(f32[64,2048]{1,0:T(8,128)S(1)} %pad_maximum_fusion.3), channel_id=1, source_target_pairs={{0,64},{64,128},{128,192},{192,256},{256,320},{320,384},{384,448},... | collective-permute-start | bytes 1572872 | tf_op jit(solution)/shard_map/ppermute | solution.py:93
  86.8 14.7 %collective-permute-start.7 = (f32[64,2048]{1,0:T(8,128)S(1)}, f32[64,2048]{1,0:T(8,128)S(1)}, u32[]{:S(2)}, u32[]{:S(2)}) collective-permute-start(f32[64,2048]{1,0:T(8,128)S(1)} %pad_maximum_fusion.2), channel_id=1, source_target_pairs={{0,64},{64,128},{128,192},{192,256},{256,320},{320,384},{384,448},... | collective-permute-start | bytes 1572872 | tf_op jit(solution)/shard_map/ppermute | solution.py:101
  93.2 14.9 %collective-permute-start.17 = (f32[64,2048]{1,0:T(8,128)S(1)}, f32[64,2048]{1,0:T(8,128)S(1)}, u32[]{:S(2)}, u32[]{:S(2)}) collective-permute-start(f32[64,2048]{1,0:T(8,128)S(1)} %pad_maximum_fusion.4), channel_id=1, source_target_pairs={{0,64},{64,128},{128,192},{192,256},{256,320},{320,384},{384,448},... | collective-permute-start | bytes 1572872 | tf_op jit(solution)/shard_map/ppermute | solution.py:101
  98.2 16.9 %collective-permute-start.12 = (f32[32,2048]{1,0:T(8,128)}, f32[32,2048]{1,0:T(8,128)S(1)}, u32[]{:S(2)}, u32[]{:S(2)}) collective-permute-start(f32[32,2048]{1,0:T(8,128)} %get-tuple-element.9), channel_id=1, source_target_pairs={{0,8},{8,0},{16,24},{24,16},{1,9},{9,1},{17,25},{25,17},{2,10},{10... | collective-permute-start | bytes 786440 | tf_op jit(solution)/shard_map/ppermute | solution.py:109
  101.7 13.4 %collective-permute-start.9 = (f32[32,2048]{1,0:T(8,128)S(1)}, f32[32,2048]{1,0:T(8,128)S(1)}, u32[]{:S(2)}, u32[]{:S(2)}) collective-permute-start(f32[32,2048]{1,0:T(8,128)S(1)} %get-tuple-element.17), channel_id=1, source_target_pairs={{0,96},{64,160},{128,224},{192,288},{256,352},{320,416},{384,480},... | collective-permute-start | bytes 786440 | tf_op jit(solution)/shard_map/ppermute | solution.py:107
  106.1 9.0 %collective-permute-start.8 = (f32[32,2048]{1,0:T(8,128)S(1)}, f32[32,2048]{1,0:T(8,128)S(1)}, u32[]{:S(2)}, u32[]{:S(2)}) collective-permute-start(f32[32,2048]{1,0:T(8,128)S(1)} %get-tuple-element.16), channel_id=1, source_target_pairs={{0,64},{64,128},{128,192},{192,256},{256,320},{320,384},{384,448},... | collective-permute-start | bytes 786440 | tf_op jit(solution)/shard_map/ppermute | solution.py:106
  108.2 11.6 %collective-permute-start.19 = (f32[32,2048]{1,0:T(8,128)S(1)}, f32[32,2048]{1,0:T(8,128)S(1)}, u32[]{:S(2)}, u32[]{:S(2)}) collective-permute-start(f32[32,2048]{1,0:T(8,128)S(1)} %get-tuple-element.21), channel_id=1, source_target_pairs={{0,104},{8,96},{16,120},{24,112},{64,168},{72,160},{80,184},{88,17... | collective-permute-start | bytes 786440 | tf_op jit(solution)/shard_map/ppermute | solution.py:111
  111.6 12.7 %collective-permute-start.18 = (f32[32,2048]{1,0:T(8,128)S(1)}, f32[32,2048]{1,0:T(8,128)S(1)}, u32[]{:S(2)}, u32[]{:S(2)}) collective-permute-start(f32[32,2048]{1,0:T(8,128)S(1)} %get-tuple-element.20), channel_id=1, source_target_pairs={{0,72},{8,64},{16,88},{24,80},{64,136},{72,128},{80,152},{88,144},... | collective-permute-start | bytes 786440 | tf_op jit(solution)/shard_map/ppermute | solution.py:110

commit v3 on v2

--- a/solution.py
+++ b/solution.py
@@ -40,12 +40,16 @@
         half = jnp.where((slot == 0) | (slot == 7), core, core ^ ((slot + 1) % 2))
         return ((y + (1 - 2 * core) * away) % ys) * 2 + half
 
-    slots = 8
-    quarter = slots * height // 2
-    lane = lax.broadcasted_iota(jnp.int32, (left.shape[0], 4 * quarter), 1)
-    source = lax.broadcasted_iota(jnp.int32, (left.shape[0], 4 * quarter), 0)
-    core = jnp.where((lane // quarter) % 2 == 0, c, 1 - c)
-    slot = (lane // (2 * quarter)) * (slots // 2) + (lane % quarter) // height
+    close, distant = 3 * height, 5 * height
+    count = 2 * (close + distant)
+    lane = lax.broadcasted_iota(jnp.int32, (left.shape[0], count), 1)
+    source = lax.broadcasted_iota(jnp.int32, (left.shape[0], count), 0)
+    late = lane >= 2 * close
+    place = jnp.where(late, lane - 2 * close, lane)
+    size = jnp.where(late, distant, close)
+    second = (place >= size).astype(jnp.int32)
+    core = c ^ second
+    slot = jnp.where(late, 3, 0) + (place - second * size) // height
     wanted = block_of(slot, core) * height + lane % height
     picked = lax.dot_general(
         left,
@@ -64,7 +68,7 @@
 
     spread = jnp.broadcast_to(picked[None], (cols,) + picked.shape)
     full = lax.all_to_all(spread, "col", split_axis=0, concat_axis=0, tiled=True)
-    full = full.reshape(rows, cols // rows * depth, 4 * quarter)
+    full = full.reshape(rows, cols // rows * depth, count)
 
     def ordered(part, at):
         order = [at, at + 2, at + 1, at - 1]
@@ -73,42 +77,41 @@
             0,
         )
 
-    near_a, far_a = full[..., : 2 * quarter], full[..., 2 * quarter :]
+    near_a, far_a = full[..., : 2 * close], full[..., 2 * close :]
     near_pair = lax.ppermute(ordered(near_a, x ^ 1), "row", swap_pair)
     far_pair = lax.ppermute(ordered(far_a, x ^ 1), "row", swap_pair)
     near_a, far_a = ordered(near_a, x), ordered(far_a, x)
 
     def product(a):
         part = dot(a, own_b)
-        other = part[quarter:]
-        return part[:quarter] + lax.ppermute(other, "layer", swap_core)
+        other = part[close:]
+        return part[:close] + lax.ppermute(other, "layer", swap_core)
 
-    def reduce(near, far):
+    part = dot(jnp.concatenate([far_a, far_pair], 1), own_b)
+    part = part.reshape(4, distant, width)
+    other = jnp.concatenate([part[1], part[3]], 0)
+    other = lax.ppermute(other, "layer", swap_core)
+    own_far, pair_far = part[0] + other[:distant], part[2] + other[distant:]
+
+    def reduce(near, far_p):
         near_p = product(near)
         total = lax.ppermute(near_p[:height], "layer", onward)
         total = jnp.concatenate(
-            [near_p[height : 2 * height] + total, near_p[2 * height : 3 * height]], 0
-        )
-        far_p = product(far)
-        total = lax.ppermute(total, "layer", onward)
-        total = jnp.concatenate(
-            [
-                total[:height] + near_p[3 * height :],
-                total[height:] + far_p[:height],
-            ],
-            0,
+            [near_p[height : 2 * height] + total, near_p[2 * height :]], 0
         )
         total = lax.ppermute(total, "layer", onward)
-        total = total + far_p[height : 3 * height]
-        return total[:height], total[height:], far_p[3 * height :]
+        total = lax.ppermute(total + far_p[: 2 * height], "layer", onward)
+        total = total + far_p[2 * height : 4 * height]
+        return total[:height], total[height:], far_p[4 * height :]
 
-    same, cross, here = reduce(near_a, far_a)
+    same, cross, here = reduce(near_a, own_far)
     here = here + lax.ppermute(same, "layer", onward)
     here = here + lax.ppermute(cross, "layer", onward_cross)
-    same, cross, there = reduce(near_pair, far_pair)
+    same, cross, there = reduce(near_pair, pair_far)
     there = lax.ppermute(there, "row", swap_pair)
-    there = there + lax.ppermute(same, ("layer", "row"), joint(onward))
-    there = there + lax.ppermute(cross, ("layer", "row"), joint(onward_cross))
+    total = jnp.concatenate([same, cross], 0)
+    total = lax.ppermute(total, ("layer", "row"), joint(onward))
+    there = there + total[:height] + lax.ppermute(total[height:], "layer", swap_core)
     return jnp.concatenate(
         [jnp.where(n == 0, here, there), jnp.where(n == 0, there, here)], 1
     )

time: 126 us -> 123 us (0.976)
  the two profiles are of different devices: /device:TPU:1 before, /device:TPU:24 now
where the time goes in v3:
time: 123 us
  starting transfers between devices  71.7 us (58%)
  waiting for transfers between devices  39.8 us (32%)
  matrix products  5.06 us (4%)
  local copies, waits for them, and re-layouts  3.26 us (3%)
  other arithmetic  2.27 us (2%)
    all_to_all x1, starting transfers between devices, body(): lax.all_to_all(spread, 'col', split_axis=0, concat_axis=0, tiled=True)  10.3 us
    ppermute x2, waiting for transfers between devices, reduce(): total = lax.ppermute(total, 'layer', onward)  9.05 us
    ppermute x2, starting transfers between devices, reduce(): total = lax.ppermute(total, 'layer', onward)  8.29 us
    ppermute x2, starting transfers between devices, reduce(): total = lax.ppermute(total + far_p[:2 * height], 'layer', onward)  7.52 us
    ppermute x2, starting transfers between devices, reduce(): total = lax.ppermute(near_p[:height], 'layer', onward)  7.28 us
    all_to_all x1, waiting for transfers between devices, body(): lax.all_to_all(spread, 'col', split_axis=0, concat_axis=0, tiled=True)  6.44 us
    ppermute x1, starting transfers between devices, body(): here = here + lax.ppermute(same, 'layer', onward)  5.59 us
    ppermute x1, starting transfers between devices, body(): total = lax.ppermute(total, ('layer', 'row'), joint(onward))  4.58 us
  transfers between devices with their start and end apart: 20, of which 11 were waited for; matrix products, arithmetic and copies ran while one was open for 6% of the time, Pallas kernels for 0%

profile of v3, /device:TPU:24, one launch (start us, length us, event | category | flops | bytes accessed | tf_op | source)
XLA Modules:
  0.0 122.8 jit_solution(6625987801232731270)
XLA Ops:
  0.1 0.8 copy-done
  0.8 0.7 convolution_bitcast_fusion
  1.6 0.9 broadcast_in_dim.33
  2.4 10.3 %all-to-all-start = ((f32[8,32,512]{2,1,0:T(8,128)}), f32[8,32,512]{2,1,0:T(8,128)S(1)}, u32[]{:S(2)}, u32[]{:S(2)}) async-start(f32[8,32,512]{2,1,0:T(8,128)} %broadcast_in_dim.33), calls=%async_computation | async-start | bytes 1048576 | tf_op jit(solution)/shard_map/all_to_all | solution.py:70
  12.7 0.1 constant_dynamic-slice_fusion.1
  12.9 3.4 %collective-permute-start.3 = (f32[64,2048]{1,0:T(8,128)S(1)}, f32[64,2048]{1,0:T(8,128)S(1)}, u32[]{:S(2)}, u32[]{:S(2)}) collective-permute-start(f32[64,2048]{1,0:T(8,128)S(1)} %get-tuple-element.12), channel_id=1, source_target_pairs={{0,8},{8,16},{16,24},{24,0},{1,9},{9,17},{17,25},{25,1},{2,10},{10... | collective-permute-start | bytes 1572872 | tf_op jit(solution)/shard_map/ppermute | solution.py:64
  16.3 3.7 %collective-permute-start.2 = (f32[64,2048]{1,0:T(8,128)S(1)}, f32[64,2048]{1,0:T(8,128)S(1)}, u32[]{:S(2)}, u32[]{:S(2)}) collective-permute-start(f32[64,2048]{1,0:T(8,128)S(1)} %get-tuple-element.12), channel_id=1, source_target_pairs={{8,0},{16,8},{24,16},{0,24},{9,1},{17,9},{25,17},{1,25},{10,2},{18... | collective-permute-start | bytes 1572872 | tf_op jit(solution)/shard_map/ppermute | solution.py:65
  19.9 3.7 %collective-permute-start.1 = (f32[64,2048]{1,0:T(8,128)S(1)}, f32[64,2048]{1,0:T(8,128)S(1)}, u32[]{:S(2)}, u32[]{:S(2)}) collective-permute-start(f32[64,2048]{1,0:T(8,128)S(1)} %get-tuple-element.11), channel_id=1, source_target_pairs={{0,16},{8,24},{16,0},{24,8},{1,17},{9,25},{17,1},{25,9},{2,18},{10... | collective-permute-start | bytes 1572872 | tf_op jit(solution)/shard_map/ppermute | solution.py:66
  23.8 6.4 %all-to-all-done = f32[8,32,512]{2,1,0:T(8,128)S(1)} async-done(((f32[8,32,512]{2,1,0:T(8,128)}), f32[8,32,512]{2,1,0:T(8,128)S(1)}, u32[]{:S(2)}, u32[]{:S(2)}) %all-to-all-start) | async-done | bytes 524320 | tf_op jit(solution)/shard_map/all_to_all | solution.py:70
  30.3 0.2 slice.119
  30.5 3.4 %collective-permute-start.12 = (f32[256,192]{1,0:T(8,128)S(1)}, f32[256,192]{1,0:T(8,128)S(1)}, u32[]{:S(2)}, u32[]{:S(2)}) collective-permute-start(f32[256,192]{1,0:T(8,128)S(1)} %pad_maximum_fusion.9), channel_id=1, source_target_pairs={{0,8},{8,0},{16,24},{24,16},{1,9},{9,1},{17,25},{25,17},{2,10},{10... | collective-permute-start | bytes 589832 | tf_op jit(solution)/shard_map/ppermute | solution.py:81
  34.0 2.4 %collective-permute-start = (f32[256,320]{1,0:T(8,128)S(1)}, f32[256,320]{1,0:T(8,128)S(1)}, u32[]{:S(2)}, u32[]{:S(2)}) collective-permute-start(f32[256,320]{1,0:T(8,128)S(1)} %pad_maximum_fusion.5), channel_id=1, source_target_pairs={{0,8},{8,0},{16,24},{24,16},{1,9},{9,1},{17,25},{25,17},{2,10},{10... | collective-permute-start | bytes 983048 | tf_op jit(solution)/shard_map/ppermute | solution.py:82
  36.5 3.7 %collective-permute-done.2 = f32[64,2048]{1,0:T(8,128)S(1)} collective-permute-done((f32[64,2048]{1,0:T(8,128)S(1)}, f32[64,2048]{1,0:T(8,128)S(1)}, u32[]{:S(2)}, u32[]{:S(2)}) %collective-permute-start.2) | collective-permute-done | bytes 524320 | tf_op jit(solution)/shard_map/ppermute | solution.py:65
  40.1 2.8 %collective-permute-done.1 = f32[64,2048]{1,0:T(8,128)S(1)} collective-permute-done((f32[64,2048]{1,0:T(8,128)S(1)}, f32[64,2048]{1,0:T(8,128)S(1)}, u32[]{:S(2)}, u32[]{:S(2)}) %collective-permute-start.1) | collective-permute-done | bytes 524320 | tf_op jit(solution)/shard_map/ppermute | solution.py:66
  43.0 0.9 fusion.51
  43.9 1.9 %collective-permute-start.5 = (f32[96,2048]{1,0:T(8,128)S(1)}, f32[96,2048]{1,0:T(8,128)S(1)}, u32[]{:S(2)}, u32[]{:S(2)}) collective-permute-start(f32[96,2048]{1,0:T(8,128)S(1)} %slice.127), channel_id=1, source_target_pairs={{0,32},{32,0},{64,96},{96,64},{128,160},{160,128},{192,224},{224,1... | collective-permute-start | bytes 2359304 | tf_op jit(solution)/shard_map/ppermute | solution.py:88
  45.9 4.0 %collective-permute-done.12 = f32[256,192]{1,0:T(8,128)S(1)} collective-permute-done((f32[256,192]{1,0:T(8,128)S(1)}, f32[256,192]{1,0:T(8,128)S(1)}, u32[]{:S(2)}, u32[]{:S(2)}) %collective-permute-start.12) | collective-permute-done | bytes 196640 | tf_op jit(solution)/shard_map/ppermute | solution.py:81
  49.9 0.9 fusion.50
  50.8 1.9 %collective-permute-start.13 = (f32[96,2048]{1,0:T(8,128)S(1)}, f32[96,2048]{1,0:T(8,128)S(1)}, u32[]{:S(2)}, u32[]{:S(2)}) collective-permute-start(f32[96,2048]{1,0:T(8,128)S(1)} %slice.139), channel_id=1, source_target_pairs={{0,32},{32,0},{64,96},{96,64},{128,160},{160,128},{192,224},{224,1... | collective-permute-start | bytes 2359304 | tf_op jit(solution)/shard_map/ppermute | solution.py:88
  52.8 3.8 %collective-permute-done = f32[256,320]{1,0:T(8,128)S(1)} collective-permute-done((f32[256,320]{1,0:T(8,128)S(1)}, f32[256,320]{1,0:T(8,128)S(1)}, u32[]{:S(2)}, u32[]{:S(2)}) %collective-permute-start) | collective-permute-done | bytes 327712 | tf_op jit(solution)/shard_map/ppermute | solution.py:82
  56.6 2.6 %fusion.20 = f32[640,2048]{1,0:T(8,128)S(1)} fusion(f32[256,320]{1,0:T(8,128)S(1)} %collective-permute-done, f32[64,320]{1,0:T(8,128)S(1)} %get-tuple-element.24, f32[64,320]{1,0:T(8,128)S(1)} %get-tuple-element.25, f32[64,320]{1,0:T(8,128)S(1)} %get-tuple-element.26, f32[64,320]{1,0:T(8,128)S(1)} %get-tuple-element.19, ...), kind=kOutput, calls=%fused_computation.46 | convolution fusion | flops 2015494144 | bytes 7995392 | tf_op jit(solution)/shard_map/dot_general | solution.py:8
  59.1 0.2 fusion.79
  59.4 0.2 pad_maximum_fusion
  59.6 1.9 %collective-permute-start.4 = (f32[320,2048]{1,0:T(8,128)S(1)}, f32[320,2048]{1,0:T(8,128)S(1)}, u32[]{:S(2)}, u32[]{:S(2)}) collective-permute-start(f32[320,2048]{1,0:T(8,128)S(1)} %pad_maximum_fusion), channel_id=1, source_target_pairs={{0,32},{32,0},{64,96},{96,64},{128,160},{160,128},{192,224},{224,1... | collective-permute-start | bytes 7864328 | tf_op jit(solution)/shard_map/ppermute | solution.py:93
  61.6 0.1 slice_add_fusion.3
  61.7 4.7 %collective-permute-start.6 = (f32[32,2048]{1,0:T(8,128)S(1)}, f32[32,2048]{1,0:T(8,128)S(1)}, u32[]{:S(2)}, u32[]{:S(2)}) collective-permute-start(f32[32,2048]{1,0:T(8,128)S(1)} %slice.129), channel_id=1, source_target_pairs={{0,64},{64,128},{128,192},{192,256},{256,320},{320,384},{384,448},... | collective-permute-start | bytes 786440 | tf_op jit(solution)/shard_map/ppermute | solution.py:98
  66.4 0.1 slice_add_fusion.2
  66.5 2.6 %collective-permute-start.14 = (f32[32,2048]{1,0:T(8,128)S(1)}, f32[32,2048]{1,0:T(8,128)S(1)}, u32[]{:S(2)}, u32[]{:S(2)}) collective-permute-start(f32[32,2048]{1,0:T(8,128)S(1)} %slice.141), channel_id=1, source_target_pairs={{0,64},{64,128},{128,192},{192,256},{256,320},{320,384},{384,448},... | collective-permute-start | bytes 786440 | tf_op jit(solution)/shard_map/ppermute | solution.py:98
  69.1 1.1 collective-permute-done.6
  70.4 5.6 %collective-permute-start.7 = (f32[64,2048]{1,0:T(8,128)S(1)}, f32[64,2048]{1,0:T(8,128)S(1)}, u32[]{:S(2)}, u32[]{:S(2)}) collective-permute-start(f32[64,2048]{1,0:T(8,128)S(1)} %pad_maximum_fusion.2), channel_id=1, source_target_pairs={{0,64},{64,128},{128,192},{192,256},{256,320},{320,384},{384,448},... | collective-permute-start | bytes 1572872 | tf_op jit(solution)/shard_map/ppermute | solution.py:102
  76.1 2.7 %collective-permute-start.15 = (f32[64,2048]{1,0:T(8,128)S(1)}, f32[64,2048]{1,0:T(8,128)S(1)}, u32[]{:S(2)}, u32[]{:S(2)}) collective-permute-start(f32[64,2048]{1,0:T(8,128)S(1)} %pad_maximum_fusion.3), channel_id=1, source_target_pairs={{0,64},{64,128},{128,192},{192,256},{256,320},{320,384},{384,448},... | collective-permute-start | bytes 1572872 | tf_op jit(solution)/shard_map/ppermute | solution.py:102
  78.8 0.4 slice_add_fusion
  79.2 9.1 %collective-permute-done.15 = f32[64,2048]{1,0:T(8,128)S(1)} collective-permute-done((f32[64,2048]{1,0:T(8,128)S(1)}, f32[64,2048]{1,0:T(8,128)S(1)}, u32[]{:S(2)}, u32[]{:S(2)}) %collective-permute-start.15) | collective-permute-done | bytes 524320 | tf_op jit(solution)/shard_map/ppermute | solution.py:102
  88.3 5.6 %collective-permute-start.16 = (f32[64,2048]{1,0:T(8,128)S(1)}, f32[64,2048]{1,0:T(8,128)S(1)}, u32[]{:S(2)}, u32[]{:S(2)}) collective-permute-start(f32[64,2048]{1,0:T(8,128)S(1)} %slice_add_fusion.5), channel_id=1, source_target_pairs={{0,64},{64,128},{128,192},{192,256},{256,320},{320,384},{384,448},... | collective-permute-start | bytes 1572872 | tf_op jit(solution)/shard_map/ppermute | solution.py:103
  93.9 0.1 slice_add_fusion.7
  94.0 1.9 %collective-permute-start.8 = (f32[64,2048]{1,0:T(8,128)S(1)}, f32[64,2048]{1,0:T(8,128)S(1)}, u32[]{:S(2)}, u32[]{:S(2)}) collective-permute-start(f32[64,2048]{1,0:T(8,128)S(1)} %slice_add_fusion.7), channel_id=1, source_target_pairs={{0,64},{64,128},{128,192},{192,256},{256,320},{320,384},{384,448},... | collective-permute-start | bytes 1572872 | tf_op jit(solution)/shard_map/ppermute | solution.py:103
  96.0 1.9 %collective-permute-start.11 = (f32[32,2048]{1,0:T(8,128)S(1)}, f32[32,2048]{1,0:T(8,128)S(1)}, u32[]{:S(2)}, u32[]{:S(2)}) collective-permute-start(f32[32,2048]{1,0:T(8,128)S(1)} %slice.137), channel_id=1, source_target_pairs={{0,8},{8,0},{16,24},{24,16},{1,9},{9,1},{17,25},{25,17},{2,10},{10... | collective-permute-start | bytes 786440 | tf_op jit(solution)/shard_map/ppermute | solution.py:111
  97.9 2.7 %collective-permute-done.16 = f32[64,2048]{1,0:T(8,128)S(1)} collective-permute-done((f32[64,2048]{1,0:T(8,128)S(1)}, f32[64,2048]{1,0:T(8,128)S(1)}, u32[]{:S(2)}, u32[]{:S(2)}) %collective-permute-start.16) | collective-permute-done | bytes 524320 | tf_op jit(solution)/shard_map/ppermute | solution.py:103
  100.7 4.6 %collective-permute-start.17 = (f32[64,2048]{1,0:T(8,128)S(1)}, f32[64,2048]{1,0:T(8,128)S(1)}, u32[]{:S(2)}, u32[]{:S(2)}) collective-permute-start(f32[64,2048]{1,0:T(8,128)S(1)} %slice_add_fusion.4), channel_id=1, source_target_pairs={{0,72},{8,64},{16,88},{24,80},{64,136},{72,128},{80,152},{88,144},... | collective-permute-start | bytes 1572872 | tf_op jit(solution)/shard_map/ppermute | solution.py:113
  105.3 1.0 collective-permute-done.8
  106.3 0.8 fusion.80
  107.1 5.6 %collective-permute-start.9 = (f32[32,2048]{1,0:T(8,128)}, f32[32,2048]{1,0:T(8,128)S(1)}, u32[]{:S(2)}, u32[]{:S(2)}) collective-permute-start(f32[32,2048]{1,0:T(8,128)} %get-tuple-element.17), channel_id=1, source_target_pairs={{0,64},{64,128},{128,192},{192,256},{256,320},{320,384},{384,448},... | collective-permute-start | bytes 786440 | tf_op jit(solution)/shard_map/ppermute | solution.py:108
  112.7 1.9 %collective-permute-start.10 = (f32[32,2048]{1,0:T(8,128)}, f32[32,2048]{1,0:T(8,128)S(1)}, u32[]{:S(2)}, u32[]{:S(2)}) collective-permute-start(f32[32,2048]{1,0:T(8,128)} %get-tuple-element.18), channel_id=1, source_target_pairs={{0,96},{64,160},{128,224},{192,288},{256,352},{320,416},{384,480},... | collective-permute-start | bytes 786440 | tf_op jit(solution)/shard_map/ppermute | solution.py:109
  114.7 1.8 %collective-permute-done.17 = f32[64,2048]{1,0:T(8,128)S(1)} collective-permute-done((f32[64,2048]{1,0:T(8,128)S(1)}, f32[64,2048]{1,0:T(8,128)S(1)}, u32[]{:S(2)}, u32[]{:S(2)}) %collective-permute-start.17) | collective-permute-done | bytes 524320 | tf_op jit(solution)/shard_map/ppermute | solution.py:113
  116.5 1.9 %collective-permute-start.18 = (f32[32,2048]{1,0:T(8,128)S(1)}, f32[32,2048]{1,0:T(8,128)S(1)}, u32[]{:S(2)}, u32[]{:S(2)}) collective-permute-start(f32[32,2048]{1,0:T(8,128)S(1)} %slice.146), channel_id=1, source_target_pairs={{0,32},{32,0},{64,96},{96,64},{128,160},{160,128},{192,224},{224,1... | collective-permute-start | bytes 786440 | tf_op jit(solution)/shard_map/ppermute | solution.py:114
  118.4 3.4 %collective-permute-done.10 = f32[32,2048]{1,0:T(8,128)S(1)} collective-permute-done((f32[32,2048]{1,0:T(8,128)}, f32[32,2048]{1,0:T(8,128)S(1)}, u32[]{:S(2)}, u32[]{:S(2)}) %collective-permute-start.10) | collective-permute-done | bytes 262176 | tf_op jit(solution)/shard_map/ppermute | solution.py:109
  121.8 0.1 broadcast_select_fusion.1
  121.9 0.8 pad_maximum_fusion.4
  (34 shorter events, 0.8 us)
Async XLA Ops:
  0.0 0.8 copy-start
  1.6 11.2 %copy-start.1 = (f32[64,4096]{1,0:T(8,128)S(1)}, f32[64,4096]{1,0:T(8,128)}, u32[]{:S(2)}) copy-start(f32[64,4096]{1,0:T(8,128)} %param.3) | copy-start | bytes 3145732
  2.4 27.8 %all-to-all-start = ((f32[8,32,512]{2,1,0:T(8,128)}), f32[8,32,512]{2,1,0:T(8,128)S(1)}, u32[]{:S(2)}, u32[]{:S(2)}) async-start(f32[8,32,512]{2,1,0:T(8,128)} %broadcast_in_dim.33), calls=%async_computation | async-start | bytes 1048576 | tf_op jit(solution)/shard_map/all_to_all | solution.py:70
  12.9 23.6 %collective-permute-start.3 = (f32[64,2048]{1,0:T(8,128)S(1)}, f32[64,2048]{1,0:T(8,128)S(1)}, u32[]{:S(2)}, u32[]{:S(2)}) collective-permute-start(f32[64,2048]{1,0:T(8,128)S(1)} %get-tuple-element.12), channel_id=1, source_target_pairs={{0,8},{8,16},{16,24},{24,0},{1,9},{9,17},{17,25},{25,1},{2,10},{10... | collective-permute-start | bytes 1572872 | tf_op jit(solution)/shard_map/ppermute | solution.py:64
  16.3 23.9 %collective-permute-start.2 = (f32[64,2048]{1,0:T(8,128)S(1)}, f32[64,2048]{1,0:T(8,128)S(1)}, u32[]{:S(2)}, u32[]{:S(2)}) collective-permute-start(f32[64,2048]{1,0:T(8,128)S(1)} %get-tuple-element.12), channel_id=1, source_target_pairs={{8,0},{16,8},{24,16},{0,24},{9,1},{17,9},{25,17},{1,25},{10,2},{18... | collective-permute-start | bytes 1572872 | tf_op jit(solution)/shard_map/ppermute | solution.py:65
  19.9 23.0 %collective-permute-start.1 = (f32[64,2048]{1,0:T(8,128)S(1)}, f32[64,2048]{1,0:T(8,128)S(1)}, u32[]{:S(2)}, u32[]{:S(2)}) collective-permute-start(f32[64,2048]{1,0:T(8,128)S(1)} %get-tuple-element.11), channel_id=1, source_target_pairs={{0,16},{8,24},{16,0},{24,8},{1,17},{9,25},{17,1},{25,9},{2,18},{10... | collective-permute-start | bytes 1572872 | tf_op jit(solution)/shard_map/ppermute | solution.py:66
  30.5 19.3 %collective-permute-start.12 = (f32[256,192]{1,0:T(8,128)S(1)}, f32[256,192]{1,0:T(8,128)S(1)}, u32[]{:S(2)}, u32[]{:S(2)}) collective-permute-start(f32[256,192]{1,0:T(8,128)S(1)} %pad_maximum_fusion.9), channel_id=1, source_target_pairs={{0,8},{8,0},{16,24},{24,16},{1,9},{9,1},{17,25},{25,17},{2,10},{10... | collective-permute-start | bytes 589832 | tf_op jit(solution)/shard_map/ppermute | solution.py:81
  34.0 22.5 %collective-permute-start = (f32[256,320]{1,0:T(8,128)S(1)}, f32[256,320]{1,0:T(8,128)S(1)}, u32[]{:S(2)}, u32[]{:S(2)}) collective-permute-start(f32[256,320]{1,0:T(8,128)S(1)} %pad_maximum_fusion.5), channel_id=1, source_target_pairs={{0,8},{8,0},{16,24},{24,16},{1,9},{9,1},{17,25},{25,17},{2,10},{10... | collective-permute-start | bytes 983048 | tf_op jit(solution)/shard_map/ppermute | solution.py:82
  43.9 17.6 %collective-permute-start.5 = (f32[96,2048]{1,0:T(8,128)S(1)}, f32[96,2048]{1,0:T(8,128)S(1)}, u32[]{:S(2)}, u32[]{:S(2)}) collective-permute-start(f32[96,2048]{1,0:T(8,128)S(1)} %slice.127), channel_id=1, source_target_pairs={{0,32},{32,0},{64,96},{96,64},{128,160},{160,128},{192,224},{224,1... | collective-permute-start | bytes 2359304 | tf_op jit(solution)/shard_map/ppermute | solution.py:88
  50.8 15.6 %collective-permute-start.13 = (f32[96,2048]{1,0:T(8,128)S(1)}, f32[96,2048]{1,0:T(8,128)S(1)}, u32[]{:S(2)}, u32[]{:S(2)}) collective-permute-start(f32[96,2048]{1,0:T(8,128)S(1)} %slice.139), channel_id=1, source_target_pairs={{0,32},{32,0},{64,96},{96,64},{128,160},{160,128},{192,224},{224,1... | collective-permute-start | bytes 2359304 | tf_op jit(solution)/shard_map/ppermute | solution.py:88
  59.6 19.1 %collective-permute-start.4 = (f32[320,2048]{1,0:T(8,128)S(1)}, f32[320,2048]{1,0:T(8,128)S(1)}, u32[]{:S(2)}, u32[]{:S(2)}) collective-permute-start(f32[320,2048]{1,0:T(8,128)S(1)} %pad_maximum_fusion), channel_id=1, source_target_pairs={{0,32},{32,0},{64,96},{96,64},{128,160},{160,128},{192,224},{224,1... | collective-permute-start | bytes 7864328 | tf_op jit(solution)/shard_map/ppermute | solution.py:93
  61.7 8.6 %collective-permute-start.6 = (f32[32,2048]{1,0:T(8,128)S(1)}, f32[32,2048]{1,0:T(8,128)S(1)}, u32[]{:S(2)}, u32[]{:S(2)}) collective-permute-start(f32[32,2048]{1,0:T(8,128)S(1)} %slice.129), channel_id=1, source_target_pairs={{0,64},{64,128},{128,192},{192,256},{256,320},{320,384},{384,448},... | collective-permute-start | bytes 786440 | tf_op jit(solution)/shard_map/ppermute | solution.py:98
  66.5 9.4 %collective-permute-start.14 = (f32[32,2048]{1,0:T(8,128)S(1)}, f32[32,2048]{1,0:T(8,128)S(1)}, u32[]{:S(2)}, u32[]{:S(2)}) collective-permute-start(f32[32,2048]{1,0:T(8,128)S(1)} %slice.141), channel_id=1, source_target_pairs={{0,64},{64,128},{128,192},{192,256},{256,320},{320,384},{384,448},... | collective-permute-start | bytes 786440 | tf_op jit(solution)/shard_map/ppermute | solution.py:98
  70.4 23.6 %collective-permute-start.7 = (f32[64,2048]{1,0:T(8,128)S(1)}, f32[64,2048]{1,0:T(8,128)S(1)}, u32[]{:S(2)}, u32[]{:S(2)}) collective-permute-start(f32[64,2048]{1,0:T(8,128)S(1)} %pad_maximum_fusion.2), channel_id=1, source_target_pairs={{0,64},{64,128},{128,192},{192,256},{256,320},{320,384},{384,448},... | collective-permute-start | bytes 1572872 | tf_op jit(solution)/shard_map/ppermute | solution.py:102
  76.1 12.2 %collective-permute-start.15 = (f32[64,2048]{1,0:T(8,128)S(1)}, f32[64,2048]{1,0:T(8,128)S(1)}, u32[]{:S(2)}, u32[]{:S(2)}) collective-permute-start(f32[64,2048]{1,0:T(8,128)S(1)} %pad_maximum_fusion.3), channel_id=1, source_target_pairs={{0,64},{64,128},{128,192},{192,256},{256,320},{320,384},{384,448},... | collective-permute-start | bytes 1572872 | tf_op jit(solution)/shard_map/ppermute | solution.py:102
  88.3 12.3 %collective-permute-start.16 = (f32[64,2048]{1,0:T(8,128)S(1)}, f32[64,2048]{1,0:T(8,128)S(1)}, u32[]{:S(2)}, u32[]{:S(2)}) collective-permute-start(f32[64,2048]{1,0:T(8,128)S(1)} %slice_add_fusion.5), channel_id=1, source_target_pairs={{0,64},{64,128},{128,192},{192,256},{256,320},{320,384},{384,448},... | collective-permute-start | bytes 1572872 | tf_op jit(solution)/shard_map/ppermute | solution.py:103
  94.0 12.2 %collective-permute-start.8 = (f32[64,2048]{1,0:T(8,128)S(1)}, f32[64,2048]{1,0:T(8,128)S(1)}, u32[]{:S(2)}, u32[]{:S(2)}) collective-permute-start(f32[64,2048]{1,0:T(8,128)S(1)} %slice_add_fusion.7), channel_id=1, source_target_pairs={{0,64},{64,128},{128,192},{192,256},{256,320},{320,384},{384,448},... | collective-permute-start | bytes 1572872 | tf_op jit(solution)/shard_map/ppermute | solution.py:103
  96.0 22.4 %collective-permute-start.11 = (f32[32,2048]{1,0:T(8,128)S(1)}, f32[32,2048]{1,0:T(8,128)S(1)}, u32[]{:S(2)}, u32[]{:S(2)}) collective-permute-start(f32[32,2048]{1,0:T(8,128)S(1)} %slice.137), channel_id=1, source_target_pairs={{0,8},{8,0},{16,24},{24,16},{1,9},{9,1},{17,25},{25,17},{2,10},{10... | collective-permute-start | bytes 786440 | tf_op jit(solution)/shard_map/ppermute | solution.py:111
  100.7 15.8 %collective-permute-start.17 = (f32[64,2048]{1,0:T(8,128)S(1)}, f32[64,2048]{1,0:T(8,128)S(1)}, u32[]{:S(2)}, u32[]{:S(2)}) collective-permute-start(f32[64,2048]{1,0:T(8,128)S(1)} %slice_add_fusion.4), channel_id=1, source_target_pairs={{0,72},{8,64},{16,88},{24,80},{64,136},{72,128},{80,152},{88,144},... | collective-permute-start | bytes 1572872 | tf_op jit(solution)/shard_map/ppermute | solution.py:113
  107.1 11.3 %collective-permute-start.9 = (f32[32,2048]{1,0:T(8,128)}, f32[32,2048]{1,0:T(8,128)S(1)}, u32[]{:S(2)}, u32[]{:S(2)}) collective-permute-start(f32[32,2048]{1,0:T(8,128)} %get-tuple-element.17), channel_id=1, source_target_pairs={{0,64},{64,128},{128,192},{192,256},{256,320},{320,384},{384,448},... | collective-permute-start | bytes 786440 | tf_op jit(solution)/shard_map/ppermute | solution.py:108
  112.7 9.1 %collective-permute-start.10 = (f32[32,2048]{1,0:T(8,128)}, f32[32,2048]{1,0:T(8,128)S(1)}, u32[]{:S(2)}, u32[]{:S(2)}) collective-permute-start(f32[32,2048]{1,0:T(8,128)} %get-tuple-element.18), channel_id=1, source_target_pairs={{0,96},{64,160},{128,224},{192,288},{256,352},{320,416},{384,480},... | collective-permute-start | bytes 786440 | tf_op jit(solution)/shard_map/ppermute | solution.py:109
  116.5 5.4 %collective-permute-start.18 = (f32[32,2048]{1,0:T(8,128)S(1)}, f32[32,2048]{1,0:T(8,128)S(1)}, u32[]{:S(2)}, u32[]{:S(2)}) collective-permute-start(f32[32,2048]{1,0:T(8,128)S(1)} %slice.146), channel_id=1, source_target_pairs={{0,32},{32,0},{64,96},{96,64},{128,160},{160,128},{192,224},{224,1... | collective-permute-start | bytes 786440 | tf_op jit(solution)/shard_map/ppermute | solution.py:114

commit v4 on v3

--- a/solution.py
+++ b/solution.py
@@ -29,7 +29,6 @@
     swap_pair = [(i, i ^ 1) for i in range(rows)]
     onward = [(2 * i, 2 * ((i + 1) % ys)) for i in range(ys)]
     onward += [(2 * i + 1, 2 * ((i - 1) % ys) + 1) for i in range(ys)]
-    onward_cross = [(i, j ^ 1) for i, j in onward]
 
     def joint(pairs):
         return [(i * rows + k, j * rows + (k ^ 1)) for i, j in pairs for k in range(rows)]
@@ -105,8 +104,8 @@
         return total[:height], total[height:], far_p[4 * height :]
 
     same, cross, here = reduce(near_a, own_far)
-    here = here + lax.ppermute(same, "layer", onward)
-    here = here + lax.ppermute(cross, "layer", onward_cross)
+    total = lax.ppermute(jnp.concatenate([same, cross], 0), "layer", onward)
+    here = here + total[:height] + lax.ppermute(total[height:], "layer", swap_core)
     same, cross, there = reduce(near_pair, pair_far)
     there = lax.ppermute(there, "row", swap_pair)
     total = jnp.concatenate([same, cross], 0)

time: 123 us -> 128 us (1.041)
  the two profiles are of different devices: /device:TPU:24 before, /device:TPU:25 now
where the time goes in v4:
time: 128 us; the launch traced here: 127 us
  starting transfers between devices  67.1 us (52%)
  waiting for transfers between devices  47.9 us (37%)
  matrix products  5.06 us (4%)
  local copies, waits for them, and re-layouts  3.85 us (3%)
  other arithmetic  2.26 us (2%)
    ppermute x2, waiting for transfers between devices, reduce(): total = lax.ppermute(total, 'layer', onward)  11.6 us
    ppermute x2, starting transfers between devices, product(): return part[:close] + lax.ppermute(other, 'layer', swap_core)  10.8 us
    ppermute x2, waiting for transfers between devices, reduce(): total = lax.ppermute(total + far_p[:2 * height], 'layer', onward)  10.8 us
    all_to_all x1, starting transfers between devices, body(): lax.all_to_all(spread, 'col', split_axis=0, concat_axis=0, tiled=True)  10 us
    ppermute x2, starting transfers between devices, body(): lax.ppermute(total[height:], 'layer', swap_core)  9.44 us
    all_to_all x1, waiting for transfers between devices, body(): lax.all_to_all(spread, 'col', split_axis=0, concat_axis=0, tiled=True)  7.74 us
    ppermute x1, waiting for transfers between devices, body(): total = lax.ppermute(total, ('layer', 'row'), joint(onward))  5.33 us
    ppermute x2, waiting for transfers between devices, reduce(): total = lax.ppermute(near_p[:height], 'layer', onward)  4.81 us
  transfers between devices with their start and end apart: 20, of which 11 were waited for; matrix products, arithmetic and copies ran while one was open for 6% of the time, Pallas kernels for 0%

profile of v4, /device:TPU:25, one launch (start us, length us, event | category | flops | bytes accessed | tf_op | source)
XLA Modules:
  0.0 126.8 jit_solution(12299649000391740940)
XLA Ops:
  0.1 0.8 copy-done
  0.8 0.7 convolution_bitcast_fusion
  1.6 0.9 broadcast_in_dim.33
  2.4 10.0 %all-to-all-start = ((f32[8,32,512]{2,1,0:T(8,128)}), f32[8,32,512]{2,1,0:T(8,128)S(1)}, u32[]{:S(2)}, u32[]{:S(2)}) async-start(f32[8,32,512]{2,1,0:T(8,128)} %broadcast_in_dim.33), calls=%async_computation | async-start | bytes 1048576 | tf_op jit(solution)/shard_map/all_to_all | solution.py:69
  12.5 0.1 constant_dynamic-slice_fusion.1
  12.6 3.1 %collective-permute-start.3 = (f32[64,2048]{1,0:T(8,128)S(1)}, f32[64,2048]{1,0:T(8,128)S(1)}, u32[]{:S(2)}, u32[]{:S(2)}) collective-permute-start(f32[64,2048]{1,0:T(8,128)S(1)} %get-tuple-element.12), channel_id=1, source_target_pairs={{0,8},{8,16},{16,24},{24,0},{1,9},{9,17},{17,25},{25,1},{2,10},{10... | collective-permute-start | bytes 1572872 | tf_op jit(solution)/shard_map/ppermute | solution.py:63
  15.7 3.4 %collective-permute-start.2 = (f32[64,2048]{1,0:T(8,128)S(1)}, f32[64,2048]{1,0:T(8,128)S(1)}, u32[]{:S(2)}, u32[]{:S(2)}) collective-permute-start(f32[64,2048]{1,0:T(8,128)S(1)} %get-tuple-element.12), channel_id=1, source_target_pairs={{8,0},{16,8},{24,16},{0,24},{9,1},{17,9},{25,17},{1,25},{10,2},{18... | collective-permute-start | bytes 1572872 | tf_op jit(solution)/shard_map/ppermute | solution.py:64
  19.1 3.4 %collective-permute-start.1 = (f32[64,2048]{1,0:T(8,128)S(1)}, f32[64,2048]{1,0:T(8,128)S(1)}, u32[]{:S(2)}, u32[]{:S(2)}) collective-permute-start(f32[64,2048]{1,0:T(8,128)S(1)} %get-tuple-element.11), channel_id=1, source_target_pairs={{0,16},{8,24},{16,0},{24,8},{1,17},{9,25},{17,1},{25,9},{2,18},{10... | collective-permute-start | bytes 1572872 | tf_op jit(solution)/shard_map/ppermute | solution.py:65
  22.7 7.7 %all-to-all-done = f32[8,32,512]{2,1,0:T(8,128)S(1)} async-done(((f32[8,32,512]{2,1,0:T(8,128)}), f32[8,32,512]{2,1,0:T(8,128)S(1)}, u32[]{:S(2)}, u32[]{:S(2)}) %all-to-all-start) | async-done | bytes 524320 | tf_op jit(solution)/shard_map/all_to_all | solution.py:69
  30.4 0.2 slice.122
  30.7 3.1 %collective-permute-start.12 = (f32[256,192]{1,0:T(8,128)S(1)}, f32[256,192]{1,0:T(8,128)S(1)}, u32[]{:S(2)}, u32[]{:S(2)}) collective-permute-start(f32[256,192]{1,0:T(8,128)S(1)} %pad_maximum_fusion.9), channel_id=1, source_target_pairs={{0,8},{8,0},{16,24},{24,16},{1,9},{9,1},{17,25},{25,17},{2,10},{10... | collective-permute-start | bytes 589832 | tf_op jit(solution)/shard_map/ppermute | solution.py:80
  33.9 2.2 %collective-permute-start = (f32[256,320]{1,0:T(8,128)S(1)}, f32[256,320]{1,0:T(8,128)S(1)}, u32[]{:S(2)}, u32[]{:S(2)}) collective-permute-start(f32[256,320]{1,0:T(8,128)S(1)} %pad_maximum_fusion.5), channel_id=1, source_target_pairs={{0,8},{8,0},{16,24},{24,16},{1,9},{9,1},{17,25},{25,17},{2,10},{10... | collective-permute-start | bytes 983048 | tf_op jit(solution)/shard_map/ppermute | solution.py:81
  36.1 4.3 %collective-permute-done.1 = f32[64,2048]{1,0:T(8,128)S(1)} collective-permute-done((f32[64,2048]{1,0:T(8,128)S(1)}, f32[64,2048]{1,0:T(8,128)S(1)}, u32[]{:S(2)}, u32[]{:S(2)}) %collective-permute-start.1) | collective-permute-done | bytes 524320 | tf_op jit(solution)/shard_map/ppermute | solution.py:65
  40.4 0.9 fusion.51
  41.4 5.1 %collective-permute-start.5 = (f32[96,2048]{1,0:T(8,128)S(1)}, f32[96,2048]{1,0:T(8,128)S(1)}, u32[]{:S(2)}, u32[]{:S(2)}) collective-permute-start(f32[96,2048]{1,0:T(8,128)S(1)} %slice.130), channel_id=1, source_target_pairs={{0,32},{32,0},{64,96},{96,64},{128,160},{160,128},{192,224},{224,1... | collective-permute-start | bytes 2359304 | tf_op jit(solution)/shard_map/ppermute | solution.py:87
  46.5 0.2 collective-permute-done.12
  46.7 0.9 fusion.50
  47.7 5.7 %collective-permute-start.13 = (f32[96,2048]{1,0:T(8,128)S(1)}, f32[96,2048]{1,0:T(8,128)S(1)}, u32[]{:S(2)}, u32[]{:S(2)}) collective-permute-start(f32[96,2048]{1,0:T(8,128)S(1)} %slice.142), channel_id=1, source_target_pairs={{0,32},{32,0},{64,96},{96,64},{128,160},{160,128},{192,224},{224,1... | collective-permute-start | bytes 2359304 | tf_op jit(solution)/shard_map/ppermute | solution.py:87
  53.4 1.7 %collective-permute-done = f32[256,320]{1,0:T(8,128)S(1)} collective-permute-done((f32[256,320]{1,0:T(8,128)S(1)}, f32[256,320]{1,0:T(8,128)S(1)}, u32[]{:S(2)}, u32[]{:S(2)}) %collective-permute-start) | collective-permute-done | bytes 327712 | tf_op jit(solution)/shard_map/ppermute | solution.py:81
  55.2 2.6 %fusion.20 = f32[640,2048]{1,0:T(8,128)S(1)} fusion(f32[256,320]{1,0:T(8,128)S(1)} %collective-permute-done, f32[64,320]{1,0:T(8,128)S(1)} %get-tuple-element.22, f32[64,320]{1,0:T(8,128)S(1)} %get-tuple-element.23, f32[64,320]{1,0:T(8,128)S(1)} %get-tuple-element.24, f32[64,320]{1,0:T(8,128)S(1)} %get-tuple-element.17, ...), kind=kOutput, calls=%fused_computation.46 | convolution fusion | flops 2015494144 | bytes 7995392 | tf_op jit(solution)/shard_map/dot_general | solution.py:8
  57.7 0.2 fusion.79
  58.0 0.2 pad_maximum_fusion
  58.2 4.0 %collective-permute-start.4 = (f32[320,2048]{1,0:T(8,128)S(1)}, f32[320,2048]{1,0:T(8,128)S(1)}, u32[]{:S(2)}, u32[]{:S(2)}) collective-permute-start(f32[320,2048]{1,0:T(8,128)S(1)} %pad_maximum_fusion), channel_id=1, source_target_pairs={{0,32},{32,0},{64,96},{96,64},{128,160},{160,128},{192,224},{224,1... | collective-permute-start | bytes 7864328 | tf_op jit(solution)/shard_map/ppermute | solution.py:92
  62.2 0.1 slice_add_fusion.3
  62.4 2.1 %collective-permute-start.6 = (f32[32,2048]{1,0:T(8,128)S(1)}, f32[32,2048]{1,0:T(8,128)S(1)}, u32[]{:S(2)}, u32[]{:S(2)}) collective-permute-start(f32[32,2048]{1,0:T(8,128)S(1)} %slice.132), channel_id=1, source_target_pairs={{0,64},{64,128},{128,192},{192,256},{256,320},{320,384},{384,448},... | collective-permute-start | bytes 786440 | tf_op jit(solution)/shard_map/ppermute | solution.py:97
  64.5 0.1 slice_add_fusion.2
  64.6 2.1 %collective-permute-start.14 = (f32[32,2048]{1,0:T(8,128)S(1)}, f32[32,2048]{1,0:T(8,128)S(1)}, u32[]{:S(2)}, u32[]{:S(2)}) collective-permute-start(f32[32,2048]{1,0:T(8,128)S(1)} %slice.144), channel_id=1, source_target_pairs={{0,64},{64,128},{128,192},{192,256},{256,320},{320,384},{384,448},... | collective-permute-start | bytes 786440 | tf_op jit(solution)/shard_map/ppermute | solution.py:97
  66.7 4.0 %collective-permute-done.6 = f32[32,2048]{1,0:T(8,128)S(1)} collective-permute-done((f32[32,2048]{1,0:T(8,128)S(1)}, f32[32,2048]{1,0:T(8,128)S(1)}, u32[]{:S(2)}, u32[]{:S(2)}) %collective-permute-start.6) | collective-permute-done | bytes 262176 | tf_op jit(solution)/shard_map/ppermute | solution.py:97
  70.8 1.9 %collective-permute-start.7 = (f32[64,2048]{1,0:T(8,128)S(1)}, f32[64,2048]{1,0:T(8,128)S(1)}, u32[]{:S(2)}, u32[]{:S(2)}) collective-permute-start(f32[64,2048]{1,0:T(8,128)S(1)} %pad_maximum_fusion.2), channel_id=1, source_target_pairs={{0,64},{64,128},{128,192},{192,256},{256,320},{320,384},{384,448},... | collective-permute-start | bytes 1572872 | tf_op jit(solution)/shard_map/ppermute | solution.py:101
  72.7 0.8 collective-permute-done.14
  73.6 1.9 %collective-permute-start.15 = (f32[64,2048]{1,0:T(8,128)S(1)}, f32[64,2048]{1,0:T(8,128)S(1)}, u32[]{:S(2)}, u32[]{:S(2)}) collective-permute-start(f32[64,2048]{1,0:T(8,128)S(1)} %pad_maximum_fusion.3), channel_id=1, source_target_pairs={{0,64},{64,128},{128,192},{192,256},{256,320},{320,384},{384,448},... | collective-permute-start | bytes 1572872 | tf_op jit(solution)/shard_map/ppermute | solution.py:101
  75.5 0.4 slice_add_fusion.1
  76.0 11.6 %collective-permute-done.15 = f32[64,2048]{1,0:T(8,128)S(1)} collective-permute-done((f32[64,2048]{1,0:T(8,128)S(1)}, f32[64,2048]{1,0:T(8,128)S(1)}, u32[]{:S(2)}, u32[]{:S(2)}) %collective-permute-start.15) | collective-permute-done | bytes 524320 | tf_op jit(solution)/shard_map/ppermute | solution.py:101
  87.6 1.9 %collective-permute-start.16 = (f32[64,2048]{1,0:T(8,128)S(1)}, f32[64,2048]{1,0:T(8,128)S(1)}, u32[]{:S(2)}, u32[]{:S(2)}) collective-permute-start(f32[64,2048]{1,0:T(8,128)S(1)} %slice_add_fusion.5), channel_id=1, source_target_pairs={{0,64},{64,128},{128,192},{192,256},{256,320},{320,384},{384,448},... | collective-permute-start | bytes 1572872 | tf_op jit(solution)/shard_map/ppermute | solution.py:102
  89.6 1.9 %collective-permute-start.8 = (f32[64,2048]{1,0:T(8,128)S(1)}, f32[64,2048]{1,0:T(8,128)S(1)}, u32[]{:S(2)}, u32[]{:S(2)}) collective-permute-start(f32[64,2048]{1,0:T(8,128)S(1)} %slice_add_fusion.7), channel_id=1, source_target_pairs={{0,64},{64,128},{128,192},{192,256},{256,320},{320,384},{384,448},... | collective-permute-start | bytes 1572872 | tf_op jit(solution)/shard_map/ppermute | solution.py:102
  91.6 7.2 %collective-permute-done.16 = f32[64,2048]{1,0:T(8,128)S(1)} collective-permute-done((f32[64,2048]{1,0:T(8,128)S(1)}, f32[64,2048]{1,0:T(8,128)S(1)}, u32[]{:S(2)}, u32[]{:S(2)}) %collective-permute-start.16) | collective-permute-done | bytes 524320 | tf_op jit(solution)/shard_map/ppermute | solution.py:102
  98.8 1.9 %collective-permute-start.17 = (f32[64,2048]{1,0:T(8,128)S(1)}, f32[64,2048]{1,0:T(8,128)S(1)}, u32[]{:S(2)}, u32[]{:S(2)}) collective-permute-start(f32[64,2048]{1,0:T(8,128)S(1)} %slice_add_fusion.4), channel_id=1, source_target_pairs={{0,72},{8,64},{16,88},{24,80},{64,136},{72,128},{80,152},{88,144},... | collective-permute-start | bytes 1572872 | tf_op jit(solution)/shard_map/ppermute | solution.py:112
  100.7 3.6 %collective-permute-done.8 = f32[64,2048]{1,0:T(8,128)S(1)} collective-permute-done((f32[64,2048]{1,0:T(8,128)S(1)}, f32[64,2048]{1,0:T(8,128)S(1)}, u32[]{:S(2)}, u32[]{:S(2)}) %collective-permute-start.8) | collective-permute-done | bytes 524320 | tf_op jit(solution)/shard_map/ppermute | solution.py:102
  104.4 1.9 %collective-permute-start.9 = (f32[64,2048]{1,0:T(8,128)S(1)}, f32[64,2048]{1,0:T(8,128)S(1)}, u32[]{:S(2)}, u32[]{:S(2)}) collective-permute-start(f32[64,2048]{1,0:T(8,128)S(1)} %slice_add_fusion.6), channel_id=1, source_target_pairs={{0,64},{64,128},{128,192},{192,256},{256,320},{320,384},{384,448},... | collective-permute-start | bytes 1572872 | tf_op jit(solution)/shard_map/ppermute | solution.py:107
  106.4 1.9 %collective-permute-start.11 = (f32[32,2048]{1,0:T(8,128)S(1)}, f32[32,2048]{1,0:T(8,128)S(1)}, u32[]{:S(2)}, u32[]{:S(2)}) collective-permute-start(f32[32,2048]{1,0:T(8,128)S(1)} %slice.140), channel_id=1, source_target_pairs={{0,8},{8,0},{16,24},{24,16},{1,9},{9,1},{17,25},{25,17},{2,10},{10... | collective-permute-start | bytes 786440 | tf_op jit(solution)/shard_map/ppermute | solution.py:110
  108.3 5.3 %collective-permute-done.17 = f32[64,2048]{1,0:T(8,128)S(1)} collective-permute-done((f32[64,2048]{1,0:T(8,128)S(1)}, f32[64,2048]{1,0:T(8,128)S(1)}, u32[]{:S(2)}, u32[]{:S(2)}) %collective-permute-start.17) | collective-permute-done | bytes 524320 | tf_op jit(solution)/shard_map/ppermute | solution.py:112
  113.6 0.7 slice.149
  114.4 5.5 %collective-permute-start.18 = (f32[32,2048]{1,0:T(8,128)}, f32[32,2048]{1,0:T(8,128)S(1)}, u32[]{:S(2)}, u32[]{:S(2)}) collective-permute-start(f32[32,2048]{1,0:T(8,128)} %slice.149), channel_id=1, source_target_pairs={{0,32},{32,0},{64,96},{96,64},{128,160},{160,128},{192,224},{224,1... | collective-permute-start | bytes 786440 | tf_op jit(solution)/shard_map/ppermute | solution.py:113
  119.9 0.7 slice.137
  120.6 4.0 %collective-permute-start.10 = (f32[32,2048]{1,0:T(8,128)}, f32[32,2048]{1,0:T(8,128)S(1)}, u32[]{:S(2)}, u32[]{:S(2)}) collective-permute-start(f32[32,2048]{1,0:T(8,128)} %slice.137), channel_id=1, source_target_pairs={{0,32},{32,0},{64,96},{96,64},{128,160},{160,128},{192,224},{224,1... | collective-permute-start | bytes 786440 | tf_op jit(solution)/shard_map/ppermute | solution.py:108
  124.6 1.3 %collective-permute-done.10 = f32[32,2048]{1,0:T(8,128)S(1)} collective-permute-done((f32[32,2048]{1,0:T(8,128)}, f32[32,2048]{1,0:T(8,128)S(1)}, u32[]{:S(2)}, u32[]{:S(2)}) %collective-permute-start.10) | collective-permute-done | bytes 262176 | tf_op jit(solution)/shard_map/ppermute | solution.py:108
  125.9 0.1 broadcast_select_fusion.1
  126.0 0.8 pad_maximum_fusion.4
  (34 shorter events, 0.9 us)
Async XLA Ops:
  0.0 0.8 copy-start
  1.6 10.9 %copy-start.1 = (f32[64,4096]{1,0:T(8,128)S(1)}, f32[64,4096]{1,0:T(8,128)}, u32[]{:S(2)}) copy-start(f32[64,4096]{1,0:T(8,128)} %param.3) | copy-start | bytes 3145732
  2.4 28.0 %all-to-all-start = ((f32[8,32,512]{2,1,0:T(8,128)}), f32[8,32,512]{2,1,0:T(8,128)S(1)}, u32[]{:S(2)}, u32[]{:S(2)}) async-start(f32[8,32,512]{2,1,0:T(8,128)} %broadcast_in_dim.33), calls=%async_computation | async-start | bytes 1048576 | tf_op jit(solution)/shard_map/all_to_all | solution.py:69
  12.6 23.5 %collective-permute-start.3 = (f32[64,2048]{1,0:T(8,128)S(1)}, f32[64,2048]{1,0:T(8,128)S(1)}, u32[]{:S(2)}, u32[]{:S(2)}) collective-permute-start(f32[64,2048]{1,0:T(8,128)S(1)} %get-tuple-element.12), channel_id=1, source_target_pairs={{0,8},{8,16},{16,24},{24,0},{1,9},{9,17},{17,25},{25,1},{2,10},{10... | collective-permute-start | bytes 1572872 | tf_op jit(solution)/shard_map/ppermute | solution.py:63
  15.7 20.4 %collective-permute-start.2 = (f32[64,2048]{1,0:T(8,128)S(1)}, f32[64,2048]{1,0:T(8,128)S(1)}, u32[]{:S(2)}, u32[]{:S(2)}) collective-permute-start(f32[64,2048]{1,0:T(8,128)S(1)} %get-tuple-element.12), channel_id=1, source_target_pairs={{8,0},{16,8},{24,16},{0,24},{9,1},{17,9},{25,17},{1,25},{10,2},{18... | collective-permute-start | bytes 1572872 | tf_op jit(solution)/shard_map/ppermute | solution.py:64
  19.1 21.3 %collective-permute-start.1 = (f32[64,2048]{1,0:T(8,128)S(1)}, f32[64,2048]{1,0:T(8,128)S(1)}, u32[]{:S(2)}, u32[]{:S(2)}) collective-permute-start(f32[64,2048]{1,0:T(8,128)S(1)} %get-tuple-element.11), channel_id=1, source_target_pairs={{0,16},{8,24},{16,0},{24,8},{1,17},{9,25},{17,1},{25,9},{2,18},{10... | collective-permute-start | bytes 1572872 | tf_op jit(solution)/shard_map/ppermute | solution.py:65
  30.7 16.0 %collective-permute-start.12 = (f32[256,192]{1,0:T(8,128)S(1)}, f32[256,192]{1,0:T(8,128)S(1)}, u32[]{:S(2)}, u32[]{:S(2)}) collective-permute-start(f32[256,192]{1,0:T(8,128)S(1)} %pad_maximum_fusion.9), channel_id=1, source_target_pairs={{0,8},{8,0},{16,24},{24,16},{1,9},{9,1},{17,25},{25,17},{2,10},{10... | collective-permute-start | bytes 589832 | tf_op jit(solution)/shard_map/ppermute | solution.py:80
  33.9 21.2 %collective-permute-start = (f32[256,320]{1,0:T(8,128)S(1)}, f32[256,320]{1,0:T(8,128)S(1)}, u32[]{:S(2)}, u32[]{:S(2)}) collective-permute-start(f32[256,320]{1,0:T(8,128)S(1)} %pad_maximum_fusion.5), channel_id=1, source_target_pairs={{0,8},{8,0},{16,24},{24,16},{1,9},{9,1},{17,25},{25,17},{2,10},{10... | collective-permute-start | bytes 983048 | tf_op jit(solution)/shard_map/ppermute | solution.py:81
  41.4 20.8 %collective-permute-start.5 = (f32[96,2048]{1,0:T(8,128)S(1)}, f32[96,2048]{1,0:T(8,128)S(1)}, u32[]{:S(2)}, u32[]{:S(2)}) collective-permute-start(f32[96,2048]{1,0:T(8,128)S(1)} %slice.130), channel_id=1, source_target_pairs={{0,32},{32,0},{64,96},{96,64},{128,160},{160,128},{192,224},{224,1... | collective-permute-start | bytes 2359304 | tf_op jit(solution)/shard_map/ppermute | solution.py:87
  47.7 16.7 %collective-permute-start.13 = (f32[96,2048]{1,0:T(8,128)S(1)}, f32[96,2048]{1,0:T(8,128)S(1)}, u32[]{:S(2)}, u32[]{:S(2)}) collective-permute-start(f32[96,2048]{1,0:T(8,128)S(1)} %slice.142), channel_id=1, source_target_pairs={{0,32},{32,0},{64,96},{96,64},{128,160},{160,128},{192,224},{224,1... | collective-permute-start | bytes 2359304 | tf_op jit(solution)/shard_map/ppermute | solution.py:87
  58.2 17.3 %collective-permute-start.4 = (f32[320,2048]{1,0:T(8,128)S(1)}, f32[320,2048]{1,0:T(8,128)S(1)}, u32[]{:S(2)}, u32[]{:S(2)}) collective-permute-start(f32[320,2048]{1,0:T(8,128)S(1)} %pad_maximum_fusion), channel_id=1, source_target_pairs={{0,32},{32,0},{64,96},{96,64},{128,160},{160,128},{192,224},{224,1... | collective-permute-start | bytes 7864328 | tf_op jit(solution)/shard_map/ppermute | solution.py:92
  62.4 8.3 %collective-permute-start.6 = (f32[32,2048]{1,0:T(8,128)S(1)}, f32[32,2048]{1,0:T(8,128)S(1)}, u32[]{:S(2)}, u32[]{:S(2)}) collective-permute-start(f32[32,2048]{1,0:T(8,128)S(1)} %slice.132), channel_id=1, source_target_pairs={{0,64},{64,128},{128,192},{192,256},{256,320},{320,384},{384,448},... | collective-permute-start | bytes 786440 | tf_op jit(solution)/shard_map/ppermute | solution.py:97
  64.6 8.9 %collective-permute-start.14 = (f32[32,2048]{1,0:T(8,128)S(1)}, f32[32,2048]{1,0:T(8,128)S(1)}, u32[]{:S(2)}, u32[]{:S(2)}) collective-permute-start(f32[32,2048]{1,0:T(8,128)S(1)} %slice.144), channel_id=1, source_target_pairs={{0,64},{64,128},{128,192},{192,256},{256,320},{320,384},{384,448},... | collective-permute-start | bytes 786440 | tf_op jit(solution)/shard_map/ppermute | solution.py:97
  70.8 18.7 %collective-permute-start.7 = (f32[64,2048]{1,0:T(8,128)S(1)}, f32[64,2048]{1,0:T(8,128)S(1)}, u32[]{:S(2)}, u32[]{:S(2)}) collective-permute-start(f32[64,2048]{1,0:T(8,128)S(1)} %pad_maximum_fusion.2), channel_id=1, source_target_pairs={{0,64},{64,128},{128,192},{192,256},{256,320},{320,384},{384,448},... | collective-permute-start | bytes 1572872 | tf_op jit(solution)/shard_map/ppermute | solution.py:101
  73.6 13.9 %collective-permute-start.15 = (f32[64,2048]{1,0:T(8,128)S(1)}, f32[64,2048]{1,0:T(8,128)S(1)}, u32[]{:S(2)}, u32[]{:S(2)}) collective-permute-start(f32[64,2048]{1,0:T(8,128)S(1)} %pad_maximum_fusion.3), channel_id=1, source_target_pairs={{0,64},{64,128},{128,192},{192,256},{256,320},{320,384},{384,448},... | collective-permute-start | bytes 1572872 | tf_op jit(solution)/shard_map/ppermute | solution.py:101
  87.6 11.1 %collective-permute-start.16 = (f32[64,2048]{1,0:T(8,128)S(1)}, f32[64,2048]{1,0:T(8,128)S(1)}, u32[]{:S(2)}, u32[]{:S(2)}) collective-permute-start(f32[64,2048]{1,0:T(8,128)S(1)} %slice_add_fusion.5), channel_id=1, source_target_pairs={{0,64},{64,128},{128,192},{192,256},{256,320},{320,384},{384,448},... | collective-permute-start | bytes 1572872 | tf_op jit(solution)/shard_map/ppermute | solution.py:102
  89.6 14.7 %collective-permute-start.8 = (f32[64,2048]{1,0:T(8,128)S(1)}, f32[64,2048]{1,0:T(8,128)S(1)}, u32[]{:S(2)}, u32[]{:S(2)}) collective-permute-start(f32[64,2048]{1,0:T(8,128)S(1)} %slice_add_fusion.7), channel_id=1, source_target_pairs={{0,64},{64,128},{128,192},{192,256},{256,320},{320,384},{384,448},... | collective-permute-start | bytes 1572872 | tf_op jit(solution)/shard_map/ppermute | solution.py:102
  98.8 14.9 %collective-permute-start.17 = (f32[64,2048]{1,0:T(8,128)S(1)}, f32[64,2048]{1,0:T(8,128)S(1)}, u32[]{:S(2)}, u32[]{:S(2)}) collective-permute-start(f32[64,2048]{1,0:T(8,128)S(1)} %slice_add_fusion.4), channel_id=1, source_target_pairs={{0,72},{8,64},{16,88},{24,80},{64,136},{72,128},{80,152},{88,144},... | collective-permute-start | bytes 1572872 | tf_op jit(solution)/shard_map/ppermute | solution.py:112
  104.4 15.4 %collective-permute-start.9 = (f32[64,2048]{1,0:T(8,128)S(1)}, f32[64,2048]{1,0:T(8,128)S(1)}, u32[]{:S(2)}, u32[]{:S(2)}) collective-permute-start(f32[64,2048]{1,0:T(8,128)S(1)} %slice_add_fusion.6), channel_id=1, source_target_pairs={{0,64},{64,128},{128,192},{192,256},{256,320},{320,384},{384,448},... | collective-permute-start | bytes 1572872 | tf_op jit(solution)/shard_map/ppermute | solution.py:107
  106.4 18.2 %collective-permute-start.11 = (f32[32,2048]{1,0:T(8,128)S(1)}, f32[32,2048]{1,0:T(8,128)S(1)}, u32[]{:S(2)}, u32[]{:S(2)}) collective-permute-start(f32[32,2048]{1,0:T(8,128)S(1)} %slice.140), channel_id=1, source_target_pairs={{0,8},{8,0},{16,24},{24,16},{1,9},{9,1},{17,25},{25,17},{2,10},{10... | collective-permute-start | bytes 786440 | tf_op jit(solution)/shard_map/ppermute | solution.py:110
  114.4 10.2 %collective-permute-start.18 = (f32[32,2048]{1,0:T(8,128)}, f32[32,2048]{1,0:T(8,128)S(1)}, u32[]{:S(2)}, u32[]{:S(2)}) collective-permute-start(f32[32,2048]{1,0:T(8,128)} %slice.149), channel_id=1, source_target_pairs={{0,32},{32,0},{64,96},{96,64},{128,160},{160,128},{192,224},{224,1... | collective-permute-start | bytes 786440 | tf_op jit(solution)/shard_map/ppermute | solution.py:113
  120.6 5.3 %collective-permute-start.10 = (f32[32,2048]{1,0:T(8,128)}, f32[32,2048]{1,0:T(8,128)S(1)}, u32[]{:S(2)}, u32[]{:S(2)}) collective-permute-start(f32[32,2048]{1,0:T(8,128)} %slice.137), channel_id=1, source_target_pairs={{0,32},{32,0},{64,96},{96,64},{128,160},{160,128},{192,224},{224,1... | collective-permute-start | bytes 786440 | tf_op jit(solution)/shard_map/ppermute | solution.py:108
